TPU v7x, 512 devices: a 8x2x16 block of a 8x8x16 slice. The times are simulated.
512 devices in a mesh: cfg: 2 (over y), ta: 8 (over x), gz: 16 (over z), gy: 2 (over core).
Axes of the slice: x: 8, y: 2, z: 16, core: 2. Of those that a mesh axis runs over, the one named last changes fastest.
The devices are a block of a 8x8x16 slice.
Arguments:
- spatial_links: float32 [6, 2, 3, 3, 16, 16, 16, 128], P('cfg', None, None, None, 'ta', 'gz', 'gy'), parts along dimension 0, may hold values from -1 to 1
- time_links: float32 [4, 3, 3, 16, 16, 16, 128], P('cfg', None, None, 'ta', 'gz', 'gy'), parts along dimension 0, may hold values from -1 to 1
Outputs:
- polyakov: float32 [4, 16, 16, 128], P('cfg', 'gz', 'gy'), parts along dimension 0
- site_mean: float32 [4], P('cfg'), parts along dimension 0
There are 2 independent parts, one for each index of `cfg`. A program takes and returns all parts, laid end to end along the dimension named above; each array names one. Nothing has to cross between parts.
All inputs are finite; a program needn't handle non-finite values.
Results may differ from a plain program's by a relative error of at most 0.0003.
Values sent between devices are 32-bit elements; how exact they have to be, the bound alone decides.
A program may use at most 64 MiB of HBM per device.

v0:
```python
from functools import partial

import jax
import jax.numpy as jnp
from jax import lax
from jax.sharding import PartitionSpec as P

ITERS = 3


smear_weight = 0.5
norm_floor = 0.25
unit_steps = ((1, 0, 0), (0, 1, 0), (0, 0, 1))


def with_halo(shard, sides, width):
    edges = {}
    for axis, dim in sides:
        devices, length = (lax.axis_size(axis), shard.shape[dim])
        up = [(i, (i + 1) % devices) for i in range(devices)]
        last = lax.slice_in_dim(shard, length - width, length, axis=dim)
        initial = lax.slice_in_dim(shard, 0, width, axis=dim)
        edges[dim] = (
            lax.ppermute(last, axis, up),
            lax.ppermute(initial, axis, [(b, a) for a, b in up]),
        )
    done = []
    for _, dim in sides:
        low, high = edges[dim]
        around = [(width, width) if d in done else (0, 0) for d in range(shard.ndim)]
        shard = jnp.concatenate([jnp.pad(low, around), shard, jnp.pad(high, around)], axis=dim)
        done.append(dim)
    return shard


def padded_2(cells, sides, width):
    for axis, dim in sides:
        count = lax.axis_size(axis)
        head = lax.slice_in_dim(cells, 0, width, axis=dim)
        tail = lax.slice_in_dim(cells, cells.shape[dim] - width, cells.shape[dim], axis=dim)
        cells = jnp.concatenate(
            [
                lax.ppermute(tail, axis, [(i, (i + 1) % count) for i in range(count)]),
                cells,
                lax.ppermute(head, axis, [((i + 1) % count, i) for i in range(count)]),
            ],
            axis=dim,
        )
    return cells


def shifted(shard, axis, by):
    devices = lax.axis_size(axis)
    return lax.ppermute(shard, axis, [(i, (i + by) % devices) for i in range(devices)])


def in_order(blocks, dim):
    blocks = jnp.moveaxis(blocks, 0, dim)
    dims = blocks.shape
    return blocks.reshape(*dims[:dim], dims[dim] * dims[dim + 1], *dims[dim + 2 :])


def sent_to_all(shard, axis):
    copies = jnp.broadcast_to(shard, (lax.axis_size(axis), *shard.shape))
    return lax.all_to_all(copies, axis, split_axis=0, concat_axis=0, tiled=True)


def gathered_copies(shard, axis, dim):
    return in_order(sent_to_all(shard, axis), dim)


def taken_together(shard, axis):
    everything = sent_to_all(shard, axis)
    return jnp.sum(everything, axis=0)


def mat_product(lhs_mat, rhs_mat):
    lhs_re = lhs_mat[0][:, :, None]
    lhs_im = lhs_mat[1][:, :, None]
    rhs_re = rhs_mat[0][None]
    rhs_im = rhs_mat[1][None]
    real_part = jnp.sum(lhs_re * rhs_re - lhs_im * rhs_im, axis=1)
    imag_part = jnp.sum(lhs_re * rhs_im + lhs_im * rhs_re, axis=1)
    return jnp.stack([real_part, imag_part])


def dagger(matrix):
    return jnp.stack([jnp.swapaxes(matrix[0], 0, 1), -jnp.swapaxes(matrix[1], 0, 1)])


def normalize_row(row_vec):
    weight = jnp.sum(row_vec[0] * row_vec[0] + row_vec[1] * row_vec[1], axis=0)
    return row_vec / jnp.sqrt(jnp.maximum(weight, norm_floor))


def project(matrix):
    first = normalize_row(matrix[:, 0])
    second_raw = matrix[:, 1]
    inner_re = jnp.sum(first[0] * second_raw[0] + first[1] * second_raw[1], axis=0)
    inner_im = jnp.sum(first[0] * second_raw[1] - first[1] * second_raw[0], axis=0)
    ortho = jnp.stack(
        [
            second_raw[0] - (inner_re * first[0] - inner_im * first[1]),
            second_raw[1] - (inner_re * first[1] + inner_im * first[0]),
        ]
    )
    second = normalize_row(ortho)
    first_one = jnp.roll(first, -1, axis=1)
    first_two = jnp.roll(first, -2, axis=1)
    second_one = jnp.roll(second, -1, axis=1)
    second_two = jnp.roll(second, -2, axis=1)
    cross_re = (
        first_one[0] * second_two[0]
        - first_one[1] * second_two[1]
        - (first_two[0] * second_one[0] - first_two[1] * second_one[1])
    )
    cross_im = (
        first_one[0] * second_two[1]
        + first_one[1] * second_two[0]
        - (first_two[0] * second_one[1] + first_two[1] * second_one[0])
    )
    third = jnp.stack([cross_re, -cross_im])
    return jnp.stack([first, second, third], axis=1)


def moved(offset, unit_vec, factor):
    return (
        offset[0] + factor * unit_vec[0],
        offset[1] + factor * unit_vec[1],
        offset[2] + factor * unit_vec[2],
    )


def smear_spatial(neighbour):
    anchor = (0, 0, 0)
    result = []
    for mu_dir in range(3):
        staples = None
        for nu_dir in range(3):
            if nu_dir == mu_dir:
                continue
            forward = unit_steps[nu_dir]
            sideways = unit_steps[mu_dir]
            upper_staple = mat_product(
                mat_product(neighbour(nu_dir, anchor), neighbour(mu_dir, forward)),
                dagger(neighbour(nu_dir, sideways)),
            )
            back_offset = moved(anchor, forward, -1)
            lower_staple = mat_product(
                mat_product(dagger(neighbour(nu_dir, back_offset)), neighbour(mu_dir, back_offset)),
                neighbour(nu_dir, moved(back_offset, sideways, 1)),
            )
            if staples is None:
                staples = upper_staple + lower_staple
            else:
                staples = staples + upper_staple + lower_staple
        mixed_link = (1.0 - smear_weight) * neighbour(mu_dir, anchor) + smear_weight / 4.0 * staples
        result.append(project(mixed_link))
    return jnp.stack(result)


def window_cut(field, offset):
    z_inner = field.shape[-3] - 2
    y_inner = field.shape[-2] - 2
    piece = field[
        ..., 1 + offset[2] : 1 + offset[2] + z_inner, 1 + offset[1] : 1 + offset[1] + y_inner, :
    ]
    return jnp.roll(piece, -offset[0], axis=-1)


def padded_neighbour(padded, direction, offset):
    return window_cut(padded[direction], offset)


def smooth_by_products(link_field, time_links, extended, depth):
    later_links = extended[0:3, :, :, :, 1 : depth + 1]
    lowers = [
        mat_product(mat_product(dagger(link_field[nu_dir]), time_links), later_links[nu_dir])
        for nu_dir in range(3)
    ]
    carried = jnp.stack([time_links] + lowers)
    padded = with_halo(carried, (("gz", 5), ("gy", 6)), 1)
    anchor = (0, 0, 0)
    staples = None
    for nu_dir in range(3):
        forward = unit_steps[nu_dir]
        upper_staple = mat_product(
            mat_product(link_field[nu_dir], window_cut(padded[0], forward)),
            dagger(later_links[nu_dir]),
        )
        lower_staple = window_cut(padded[1 + nu_dir], moved(anchor, forward, -1))
        if staples is None:
            staples = upper_staple + lower_staple
        else:
            staples = staples + upper_staple + lower_staple
    mixed_link = (1.0 - smear_weight) * time_links + smear_weight / 6.0 * staples
    return project(mixed_link)


def on_device(spatial_links, time_links):
    link_field = spatial_links
    for sweep_index in range(ITERS):
        padded = padded_2(link_field, (("gz", 5), ("gy", 6)), 1)
        link_field = smear_spatial(partial(padded_neighbour, padded))
    stacked = jnp.concatenate([link_field, time_links[None]], axis=0)
    ahead_slice = shifted(stacked[:, :, :, :, 0:1], "ta", -1)
    extended = jnp.concatenate([stacked, ahead_slice], axis=4)
    depth = time_links.shape[3]
    smoothed = smooth_by_products(link_field, time_links, extended, depth)
    block_prod = smoothed[:, :, :, 0]
    block_prod = mat_product(block_prod, smoothed[:, :, :, 1])
    pieces = gathered_copies(block_prod[None], "ta", 0)

    def advance(index, carry):
        return mat_product(carry, pieces[index])

    whole_prod = lax.fori_loop(1, pieces.shape[0], advance, pieces[0])
    polyakov = (
        jnp.stack(
            [
                whole_prod[0, 0, 0] + whole_prod[0, 1, 1] + whole_prod[0, 2, 2],
                whole_prod[1, 0, 0] + whole_prod[1, 1, 1] + whole_prod[1, 2, 2],
            ]
        )
        / 3.0
    )
    local_sums = jnp.sum(polyakov, axis=(1, 2, 3))
    totals = taken_together(local_sums, ("gz", "gy"))
    site_count = (
        polyakov.shape[1]
        * polyakov.shape[2]
        * polyakov.shape[3]
        * lax.axis_size("gz")
        * lax.axis_size("gy")
    )
    site_mean = totals / site_count
    return (polyakov, site_mean)


def solution(mesh):
    placed = (
        P("cfg", None, None, None, "ta", "gz", "gy", None),
        P("cfg", None, None, "ta", "gz", "gy", None),
    )
    return jax.shard_map(
        on_device,
        mesh=mesh,
        in_specs=placed,
        out_specs=(P("cfg", "gz", "gy", None), P("cfg")),
        check_vma=False,
    )
```

profile of v0, /device:TPU:65, one launch (start us, length us, event | category | flops | bytes accessed | tf_op | source)
XLA Modules:
  0.0 209.3 jit_solution(16475524632633081264)
XLA Ops:
  0.6 1.0 copy.350
  1.7 6.6 %collective-permute-start = (f32[3,2,3,3,2,1,8,128]{7,6,4,3,1,2,5,0:T(8,128)S(1)}, f32[3,2,3,3,2,1,8,128]{7,6,4,3,1,2,5,0:T(8,128)S(1)}, u32[]{:S(2)}, u32[]{:S(2)}) collective-permute-start(f32[3,2,3,3,2,1,8,128]{7,6,4,3,1,2,5,0:T(8,128)S(1)} %copy.350), channel_id=1, source_target_pairs={{0,2},{2,4},{4,6},{6,8},{8,10},{10,12},{12,14},{14,16},{16,18},{18... | collective-permute-start | bytes 1327112 | tf_op jit(solution)/shard_map/ppermute | solution.py:43
  8.3 39.9 %collective-permute-start.1 = (f32[3,2,3,3,2,1,8,128]{7,6,4,3,1,2,5,0:T(8,128)S(1)}, f32[3,2,3,3,2,1,8,128]{7,6,4,3,1,2,5,0:T(8,128)S(1)}, u32[]{:S(2)}, u32[]{:S(2)}) collective-permute-start(f32[3,2,3,3,2,1,8,128]{7,6,4,3,1,2,5,0:T(8,128)S(1)} %copy.350), channel_id=1, source_target_pairs={{2,0},{4,2},{6,4},{8,6},{10,8},{12,10},{14,12},{16,14},{18,16},{20... | collective-permute-start | bytes 1327112 | tf_op jit(solution)/shard_map/ppermute | solution.py:45
  48.2 6.8 %collective-permute-done = f32[3,2,3,3,2,1,8,128]{7,6,4,3,1,2,5,0:T(8,128)S(1)} collective-permute-done((f32[3,2,3,3,2,1,8,128]{7,6,4,3,1,2,5,0:T(8,128)S(1)}, f32[3,2,3,3,2,1,8,128]{7,6,4,3,1,2,5,0:T(8,128)S(1)}, u32[]{:S(2)}, u32[]{:S(2)}) %collective-permute-start) | collective-permute-done | bytes 442400 | tf_op jit(solution)/shard_map/ppermute | solution.py:43
  55.1 1.0 constant_dynamic-update-slice_fusion.1
  56.2 0.2 fusion.300
  56.4 4.4 %collective-permute-start.2 = (f32[3,2,3,3,2,3,1,128]{7,6,4,3,1,2,5,0:T(1,128)S(1)}, f32[3,2,3,3,2,3,1,128]{7,6,4,3,1,2,5,0:T(1,128)S(1)}, u32[]{:S(2)}, u32[]{:S(2)}) collective-permute-start(f32[3,2,3,3,2,3,1,128]{7,6,4,3,1,2,5,0:T(1,128)S(1)} %get-tuple-element.379), channel_id=1, source_target_pairs={{0,1},{1,0},{2,3},{3,2},{4,5},{5,4},{6,7},{7,6},{8,9},{9,8},{10,11... | collective-permute-start | bytes 497672 | tf_op jit(solution)/shard_map/ppermute | solution.py:43
  60.8 2.0 collective-permute-start.3
  62.7 1.4 collective-permute-done.3
  64.1 0.5 pad_maximum_fusion.1
  64.6 0.4 slice_bitcast_fusion.13
  65.1 0.1 fusion.315
  65.5 0.1 fusion.313
  66.5 0.1 subtract_reduce_fusion.80
  67.5 0.2 fusion.317
  68.6 0.1 subtract_reduce_fusion.76
  69.1 0.2 fusion.9
  70.0 2.0 collective-permute-start.4
  71.9 5.4 %collective-permute-start.5 = (f32[3,2,3,3,2,1,8,128]{7,6,4,3,1,2,5,0:T(8,128)S(1)}, f32[3,2,3,3,2,1,8,128]{7,6,4,3,1,2,5,0:T(8,128)S(1)}, u32[]{:S(2)}, u32[]{:S(2)}) collective-permute-start(f32[3,2,3,3,2,1,8,128]{7,6,4,3,1,2,5,0:T(8,128)S(1)} %pad_maximum_fusion.5), channel_id=1, source_target_pairs={{2,0},{4,2},{6,4},{8,6},{10,8},{12,10},{14,12},{16,14},{18,16},{20... | collective-permute-start | bytes 1327112 | tf_op jit(solution)/shard_map/ppermute | solution.py:45
  77.3 8.4 %collective-permute-done.4 = f32[3,2,3,3,2,1,8,128]{7,6,4,3,1,2,5,0:T(8,128)S(1)} collective-permute-done((f32[3,2,3,3,2,1,8,128]{7,6,4,3,1,2,5,0:T(8,128)S(1)}, f32[3,2,3,3,2,1,8,128]{7,6,4,3,1,2,5,0:T(8,128)S(1)}, u32[]{:S(2)}, u32[]{:S(2)}) %collective-permute-start.4) | collective-permute-done | bytes 442400 | tf_op jit(solution)/shard_map/ppermute | solution.py:43
  85.7 0.9 collective-permute-done.5
  86.7 0.2 pad_maximum_fusion.19
  86.9 2.9 %collective-permute-start.6 = (f32[3,2,3,3,2,3,1,128]{7,6,4,3,1,2,5,0:T(1,128)S(1)}, f32[3,2,3,3,2,3,1,128]{7,6,4,3,1,2,5,0:T(1,128)S(1)}, u32[]{:S(2)}, u32[]{:S(2)}) collective-permute-start(f32[3,2,3,3,2,3,1,128]{7,6,4,3,1,2,5,0:T(1,128)S(1)} %get-tuple-element.377), channel_id=1, source_target_pairs={{0,1},{1,0},{2,3},{3,2},{4,5},{5,4},{6,7},{7,6},{8,9},{9,8},{10,11... | collective-permute-start | bytes 497672 | tf_op jit(solution)/shard_map/ppermute | solution.py:43
  89.8 2.0 collective-permute-start.7
  91.8 1.4 collective-permute-done.7
  93.1 0.5 pad_maximum_fusion.2
  93.6 0.4 slice_bitcast_fusion.10
  94.1 0.1 fusion.309
  94.5 0.1 fusion.307
  95.7 0.1 subtract_reduce_fusion.56
  96.6 0.2 fusion.311
  99.3 2.0 collective-permute-start.8
  101.2 5.4 %collective-permute-start.9 = (f32[3,2,3,3,2,1,8,128]{7,6,4,3,1,2,5,0:T(8,128)S(1)}, f32[3,2,3,3,2,1,8,128]{7,6,4,3,1,2,5,0:T(8,128)S(1)}, u32[]{:S(2)}, u32[]{:S(2)}) collective-permute-start(f32[3,2,3,3,2,1,8,128]{7,6,4,3,1,2,5,0:T(8,128)S(1)} %pad_maximum_fusion.6), channel_id=1, source_target_pairs={{2,0},{4,2},{6,4},{8,6},{10,8},{12,10},{14,12},{16,14},{18,16},{20... | collective-permute-start | bytes 1327112 | tf_op jit(solution)/shard_map/ppermute | solution.py:45
  106.6 8.4 %collective-permute-done.8 = f32[3,2,3,3,2,1,8,128]{7,6,4,3,1,2,5,0:T(8,128)S(1)} collective-permute-done((f32[3,2,3,3,2,1,8,128]{7,6,4,3,1,2,5,0:T(8,128)S(1)}, f32[3,2,3,3,2,1,8,128]{7,6,4,3,1,2,5,0:T(8,128)S(1)}, u32[]{:S(2)}, u32[]{:S(2)}) %collective-permute-start.8) | collective-permute-done | bytes 442400 | tf_op jit(solution)/shard_map/ppermute | solution.py:43
  115.0 0.9 collective-permute-done.9
  116.0 0.2 pad_maximum_fusion.14
  116.2 2.9 %collective-permute-start.10 = (f32[3,2,3,3,2,3,1,128]{7,6,4,3,1,2,5,0:T(1,128)S(1)}, f32[3,2,3,3,2,3,1,128]{7,6,4,3,1,2,5,0:T(1,128)S(1)}, u32[]{:S(2)}, u32[]{:S(2)}) collective-permute-start(f32[3,2,3,3,2,3,1,128]{7,6,4,3,1,2,5,0:T(1,128)S(1)} %get-tuple-element.375), channel_id=1, source_target_pairs={{0,1},{1,0},{2,3},{3,2},{4,5},{5,4},{6,7},{7,6},{8,9},{9,8},{10,11... | collective-permute-start | bytes 497672 | tf_op jit(solution)/shard_map/ppermute | solution.py:43
  119.1 2.1 %collective-permute-start.11 = (f32[3,2,3,3,2,3,1,128]{7,6,4,3,1,2,5,0:T(1,128)S(1)}, f32[3,2,3,3,2,3,1,128]{7,6,4,3,1,2,5,0:T(1,128)S(1)}, u32[]{:S(2)}, u32[]{:S(2)}) collective-permute-start(f32[3,2,3,3,2,3,1,128]{7,6,4,3,1,2,5,0:T(1,128)S(1)} %get-tuple-element.376), channel_id=1, source_target_pairs={{1,0},{0,1},{3,2},{2,3},{5,4},{4,5},{7,6},{6,7},{9,8},{8,9},{11,10... | collective-permute-start | bytes 497672 | tf_op jit(solution)/shard_map/ppermute | solution.py:45
  121.3 1.2 collective-permute-done.11
  122.4 0.5 pad_maximum_fusion.3
  122.9 0.4 slice_bitcast_fusion.7
  123.4 0.1 fusion.303
  123.8 0.1 fusion.301
  125.8 0.2 fusion.305
  128.5 5.5 %collective-permute-start.12 = (f32[4,2,3,3,1,1,8,128]{7,6,4,3,1,2,5,0:T(8,128)S(1)}, f32[4,2,3,3,1,1,8,128]{7,6,4,3,1,2,5,0:T(8,128)S(1)}, u32[]{:S(2)}, u32[]{:S(2)}) collective-permute-start(f32[4,2,3,3,1,1,8,128]{7,6,4,3,1,2,5,0:T(8,128)S(1)} %pad_maximum_fusion.7), channel_id=1, source_target_pairs={{0,224},{32,0},{64,32},{96,64},{128,96},{160,128},{192,160},{224,1... | collective-permute-start | bytes 884744 | tf_op jit(solution)/shard_map/ppermute | solution.py:54
  134.1 0.2 subtract_reduce_fusion.28
  134.3 5.9 %collective-permute-done.12 = f32[4,2,3,3,1,1,8,128]{7,6,4,3,1,2,5,0:T(8,128)S(1)} collective-permute-done((f32[4,2,3,3,1,1,8,128]{7,6,4,3,1,2,5,0:T(8,128)S(1)}, f32[4,2,3,3,1,1,8,128]{7,6,4,3,1,2,5,0:T(8,128)S(1)}, u32[]{:S(2)}, u32[]{:S(2)}) %collective-permute-start.12) | collective-permute-done | bytes 294944 | tf_op jit(solution)/shard_map/ppermute | solution.py:54
  140.6 2.0 collective-permute-start.14
  142.5 5.4 %collective-permute-start.15 = (f32[4,2,3,3,2,1,8,128]{7,6,4,3,1,2,5,0:T(8,128)S(1)}, f32[4,2,3,3,2,1,8,128]{7,6,4,3,1,2,5,0:T(8,128)S(1)}, u32[]{:S(2)}, u32[]{:S(2)}) collective-permute-start(f32[4,2,3,3,2,1,8,128]{7,6,4,3,1,2,5,0:T(8,128)S(1)} %pad_maximum_fusion.4), channel_id=1, source_target_pairs={{2,0},{4,2},{6,4},{8,6},{10,8},{12,10},{14,12},{16,14},{18,16},{20... | collective-permute-start | bytes 1769480 | tf_op jit(solution)/shard_map/ppermute | solution.py:25
  148.0 3.2 %collective-permute-start.13 = (f32[4,2,3,3,2,1,1,128]{7,6,4,3,1,2,5,0:T(1,128)S(1)}, f32[4,2,3,3,2,1,1,128]{7,6,4,3,1,2,5,0:T(1,128)S(1)}, u32[]{:S(2)}, u32[]{:S(2)}) collective-permute-start(f32[4,2,3,3,2,1,1,128]{7,6,4,3,1,2,5,0:T(1,128)S(1)} %get-tuple-element.560), channel_id=1, source_target_pairs={{0,1},{1,0},{2,3},{3,2},{4,5},{5,4},{6,7},{7,6},{8,9},{9,8},{10,11... | collective-permute-start | bytes 221192 | tf_op jit(solution)/shard_map/ppermute | solution.py:24
  151.2 2.0 collective-permute-start.16
  153.2 1.2 collective-permute-done.16
  154.4 4.2 %collective-permute-done.14 = f32[4,2,3,3,2,1,8,128]{7,6,4,3,1,2,5,0:T(8,128)S(1)} collective-permute-done((f32[4,2,3,3,2,1,8,128]{7,6,4,3,1,2,5,0:T(8,128)S(1)}, f32[4,2,3,3,2,1,8,128]{7,6,4,3,1,2,5,0:T(8,128)S(1)}, u32[]{:S(2)}, u32[]{:S(2)}) %collective-permute-start.14) | collective-permute-done | bytes 589856 | tf_op jit(solution)/shard_map/ppermute | solution.py:24
  158.6 0.9 collective-permute-done.15
  159.6 0.7 select_maximum_fusion
  160.3 0.5 slice_bitcast_fusion.4
  161.7 0.1 fusion.1
  162.2 0.8 broadcast_in_dim.4
  163.1 5.7 %all-to-all-start = ((f32[8,1,2,3,3,1,8,128]{7,6,4,3,2,5,1,0:T(8,128)}), f32[8,1,2,3,3,1,8,128]{7,6,4,3,2,5,1,0:T(8,128)S(1)}, u32[]{:S(2)}, u32[]{:S(2)}) async-start(f32[8,1,2,3,3,1,8,128]{7,6,4,3,2,5,1,0:T(8,128)} %broadcast_in_dim.4), calls=%async_computation | async-start | bytes 1179648 | tf_op jit(solution)/shard_map/all_to_all | solution.py:65
  168.8 17.2 %all-to-all-done = f32[8,1,2,3,3,1,8,128]{7,6,4,3,2,5,1,0:T(8,128)S(1)} async-done(((f32[8,1,2,3,3,1,8,128]{7,6,4,3,2,5,1,0:T(8,128)}), f32[8,1,2,3,3,1,8,128]{7,6,4,3,2,5,1,0:T(8,128)S(1)}, u32[]{:S(2)}, u32[]{:S(2)}) %all-to-all-start) | async-done | bytes 589856 | tf_op jit(solution)/shard_map/all_to_all | solution.py:65
  185.9 0.8 while.15
  186.7 0.6 fusion.299
  187.3 21.4 %all_to_all.11 = f32[32,1,2]{2,1,0:T(1,128)S(1)} all-to-all(f32[32,1,2]{2,1,0:T(1,128)S(1)} %broadcast_in_dim.5), channel_id=1, replica_groups=mesh['cfg'=2,'ta'=8,'gz'=16,'gy'=2] {'gz','gy'}, dimensions={0} | all-to-all | bytes 512 | tf_op jit(solution)/shard_map/all_to_all | solution.py:65
  208.8 0.5 broadcast_multiply_fusion
  (361 shorter events, 13.7 us)
Async XLA Ops:
  1.7 53.3 %collective-permute-start = (f32[3,2,3,3,2,1,8,128]{7,6,4,3,1,2,5,0:T(8,128)S(1)}, f32[3,2,3,3,2,1,8,128]{7,6,4,3,1,2,5,0:T(8,128)S(1)}, u32[]{:S(2)}, u32[]{:S(2)}) collective-permute-start(f32[3,2,3,3,2,1,8,128]{7,6,4,3,1,2,5,0:T(8,128)S(1)} %copy.350), channel_id=1, source_target_pairs={{0,2},{2,4},{4,6},{6,8},{8,10},{10,12},{12,14},{14,16},{16,18},{18... | collective-permute-start | bytes 1327112 | tf_op jit(solution)/shard_map/ppermute | solution.py:43
  8.3 47.9 %collective-permute-start.1 = (f32[3,2,3,3,2,1,8,128]{7,6,4,3,1,2,5,0:T(8,128)S(1)}, f32[3,2,3,3,2,1,8,128]{7,6,4,3,1,2,5,0:T(8,128)S(1)}, u32[]{:S(2)}, u32[]{:S(2)}) collective-permute-start(f32[3,2,3,3,2,1,8,128]{7,6,4,3,1,2,5,0:T(8,128)S(1)} %copy.350), channel_id=1, source_target_pairs={{2,0},{4,2},{6,4},{8,6},{10,8},{12,10},{14,12},{16,14},{18,16},{20... | collective-permute-start | bytes 1327112 | tf_op jit(solution)/shard_map/ppermute | solution.py:45
  56.4 6.3 %collective-permute-start.2 = (f32[3,2,3,3,2,3,1,128]{7,6,4,3,1,2,5,0:T(1,128)S(1)}, f32[3,2,3,3,2,3,1,128]{7,6,4,3,1,2,5,0:T(1,128)S(1)}, u32[]{:S(2)}, u32[]{:S(2)}) collective-permute-start(f32[3,2,3,3,2,3,1,128]{7,6,4,3,1,2,5,0:T(1,128)S(1)} %get-tuple-element.379), channel_id=1, source_target_pairs={{0,1},{1,0},{2,3},{3,2},{4,5},{5,4},{6,7},{7,6},{8,9},{9,8},{10,11... | collective-permute-start | bytes 497672 | tf_op jit(solution)/shard_map/ppermute | solution.py:43
  60.8 3.3 %collective-permute-start.3 = (f32[3,2,3,3,2,3,1,128]{7,6,4,3,1,2,5,0:T(1,128)S(1)}, f32[3,2,3,3,2,3,1,128]{7,6,4,3,1,2,5,0:T(1,128)S(1)}, u32[]{:S(2)}, u32[]{:S(2)}) collective-permute-start(f32[3,2,3,3,2,3,1,128]{7,6,4,3,1,2,5,0:T(1,128)S(1)} %get-tuple-element.380), channel_id=1, source_target_pairs={{1,0},{0,1},{3,2},{2,3},{5,4},{4,5},{7,6},{6,7},{9,8},{8,9},{11,10... | collective-permute-start | bytes 497672 | tf_op jit(solution)/shard_map/ppermute | solution.py:45
  70.0 15.7 %collective-permute-start.4 = (f32[3,2,3,3,2,1,8,128]{7,6,4,3,1,2,5,0:T(8,128)S(1)}, f32[3,2,3,3,2,1,8,128]{7,6,4,3,1,2,5,0:T(8,128)S(1)}, u32[]{:S(2)}, u32[]{:S(2)}) collective-permute-start(f32[3,2,3,3,2,1,8,128]{7,6,4,3,1,2,5,0:T(8,128)S(1)} %pad_maximum_fusion.5), channel_id=1, source_target_pairs={{0,2},{2,4},{4,6},{6,8},{8,10},{10,12},{12,14},{14,16},{16,18},{18... | collective-permute-start | bytes 1327112 | tf_op jit(solution)/shard_map/ppermute | solution.py:43
  71.9 14.7 %collective-permute-start.5 = (f32[3,2,3,3,2,1,8,128]{7,6,4,3,1,2,5,0:T(8,128)S(1)}, f32[3,2,3,3,2,1,8,128]{7,6,4,3,1,2,5,0:T(8,128)S(1)}, u32[]{:S(2)}, u32[]{:S(2)}) collective-permute-start(f32[3,2,3,3,2,1,8,128]{7,6,4,3,1,2,5,0:T(8,128)S(1)} %pad_maximum_fusion.5), channel_id=1, source_target_pairs={{2,0},{4,2},{6,4},{8,6},{10,8},{12,10},{14,12},{16,14},{18,16},{20... | collective-permute-start | bytes 1327112 | tf_op jit(solution)/shard_map/ppermute | solution.py:45
  86.9 4.9 %collective-permute-start.6 = (f32[3,2,3,3,2,3,1,128]{7,6,4,3,1,2,5,0:T(1,128)S(1)}, f32[3,2,3,3,2,3,1,128]{7,6,4,3,1,2,5,0:T(1,128)S(1)}, u32[]{:S(2)}, u32[]{:S(2)}) collective-permute-start(f32[3,2,3,3,2,3,1,128]{7,6,4,3,1,2,5,0:T(1,128)S(1)} %get-tuple-element.377), channel_id=1, source_target_pairs={{0,1},{1,0},{2,3},{3,2},{4,5},{5,4},{6,7},{7,6},{8,9},{9,8},{10,11... | collective-permute-start | bytes 497672 | tf_op jit(solution)/shard_map/ppermute | solution.py:43
  89.8 3.3 %collective-permute-start.7 = (f32[3,2,3,3,2,3,1,128]{7,6,4,3,1,2,5,0:T(1,128)S(1)}, f32[3,2,3,3,2,3,1,128]{7,6,4,3,1,2,5,0:T(1,128)S(1)}, u32[]{:S(2)}, u32[]{:S(2)}) collective-permute-start(f32[3,2,3,3,2,3,1,128]{7,6,4,3,1,2,5,0:T(1,128)S(1)} %get-tuple-element.378), channel_id=1, source_target_pairs={{1,0},{0,1},{3,2},{2,3},{5,4},{4,5},{7,6},{6,7},{9,8},{8,9},{11,10... | collective-permute-start | bytes 497672 | tf_op jit(solution)/shard_map/ppermute | solution.py:45
  98.7 7.9 %copy-start = (f32[2,3,3,2,1,8,128]{6,5,4,3,2,1,0:T(8,128)S(1)}, f32[2,3,3,2,1,8,128]{6,5,4,3,2,1,0:T(8,128)}, u32[]{:S(2)}) copy-start(f32[2,3,3,2,1,8,128]{6,5,4,3,2,1,0:T(8,128)} %param.5) | copy-start | bytes 442372
  99.3 15.7 %collective-permute-start.8 = (f32[3,2,3,3,2,1,8,128]{7,6,4,3,1,2,5,0:T(8,128)S(1)}, f32[3,2,3,3,2,1,8,128]{7,6,4,3,1,2,5,0:T(8,128)S(1)}, u32[]{:S(2)}, u32[]{:S(2)}) collective-permute-start(f32[3,2,3,3,2,1,8,128]{7,6,4,3,1,2,5,0:T(8,128)S(1)} %pad_maximum_fusion.6), channel_id=1, source_target_pairs={{0,2},{2,4},{4,6},{6,8},{8,10},{10,12},{12,14},{14,16},{16,18},{18... | collective-permute-start | bytes 1327112 | tf_op jit(solution)/shard_map/ppermute | solution.py:43
  101.2 14.7 %collective-permute-start.9 = (f32[3,2,3,3,2,1,8,128]{7,6,4,3,1,2,5,0:T(8,128)S(1)}, f32[3,2,3,3,2,1,8,128]{7,6,4,3,1,2,5,0:T(8,128)S(1)}, u32[]{:S(2)}, u32[]{:S(2)}) collective-permute-start(f32[3,2,3,3,2,1,8,128]{7,6,4,3,1,2,5,0:T(8,128)S(1)} %pad_maximum_fusion.6), channel_id=1, source_target_pairs={{2,0},{4,2},{6,4},{8,6},{10,8},{12,10},{14,12},{16,14},{18,16},{20... | collective-permute-start | bytes 1327112 | tf_op jit(solution)/shard_map/ppermute | solution.py:45
  116.2 5.1 %collective-permute-start.10 = (f32[3,2,3,3,2,3,1,128]{7,6,4,3,1,2,5,0:T(1,128)S(1)}, f32[3,2,3,3,2,3,1,128]{7,6,4,3,1,2,5,0:T(1,128)S(1)}, u32[]{:S(2)}, u32[]{:S(2)}) collective-permute-start(f32[3,2,3,3,2,3,1,128]{7,6,4,3,1,2,5,0:T(1,128)S(1)} %get-tuple-element.375), channel_id=1, source_target_pairs={{0,1},{1,0},{2,3},{3,2},{4,5},{5,4},{6,7},{7,6},{8,9},{9,8},{10,11... | collective-permute-start | bytes 497672 | tf_op jit(solution)/shard_map/ppermute | solution.py:43
  119.1 3.3 %collective-permute-start.11 = (f32[3,2,3,3,2,3,1,128]{7,6,4,3,1,2,5,0:T(1,128)S(1)}, f32[3,2,3,3,2,3,1,128]{7,6,4,3,1,2,5,0:T(1,128)S(1)}, u32[]{:S(2)}, u32[]{:S(2)}) collective-permute-start(f32[3,2,3,3,2,3,1,128]{7,6,4,3,1,2,5,0:T(1,128)S(1)} %get-tuple-element.376), channel_id=1, source_target_pairs={{1,0},{0,1},{3,2},{2,3},{5,4},{4,5},{7,6},{6,7},{9,8},{8,9},{11,10... | collective-permute-start | bytes 497672 | tf_op jit(solution)/shard_map/ppermute | solution.py:45
  128.5 11.7 %collective-permute-start.12 = (f32[4,2,3,3,1,1,8,128]{7,6,4,3,1,2,5,0:T(8,128)S(1)}, f32[4,2,3,3,1,1,8,128]{7,6,4,3,1,2,5,0:T(8,128)S(1)}, u32[]{:S(2)}, u32[]{:S(2)}) collective-permute-start(f32[4,2,3,3,1,1,8,128]{7,6,4,3,1,2,5,0:T(8,128)S(1)} %pad_maximum_fusion.7), channel_id=1, source_target_pairs={{0,224},{32,0},{64,32},{96,64},{128,96},{160,128},{192,160},{224,1... | collective-permute-start | bytes 884744 | tf_op jit(solution)/shard_map/ppermute | solution.py:54
  140.6 18.1 %collective-permute-start.14 = (f32[4,2,3,3,2,1,8,128]{7,6,4,3,1,2,5,0:T(8,128)S(1)}, f32[4,2,3,3,2,1,8,128]{7,6,4,3,1,2,5,0:T(8,128)S(1)}, u32[]{:S(2)}, u32[]{:S(2)}) collective-permute-start(f32[4,2,3,3,2,1,8,128]{7,6,4,3,1,2,5,0:T(8,128)S(1)} %pad_maximum_fusion.4), channel_id=1, source_target_pairs={{0,2},{2,4},{4,6},{6,8},{8,10},{10,12},{12,14},{14,16},{16,18},{18... | collective-permute-start | bytes 1769480 | tf_op jit(solution)/shard_map/ppermute | solution.py:24
  142.5 17.0 %collective-permute-start.15 = (f32[4,2,3,3,2,1,8,128]{7,6,4,3,1,2,5,0:T(8,128)S(1)}, f32[4,2,3,3,2,1,8,128]{7,6,4,3,1,2,5,0:T(8,128)S(1)}, u32[]{:S(2)}, u32[]{:S(2)}) collective-permute-start(f32[4,2,3,3,2,1,8,128]{7,6,4,3,1,2,5,0:T(8,128)S(1)} %pad_maximum_fusion.4), channel_id=1, source_target_pairs={{2,0},{4,2},{6,4},{8,6},{10,8},{12,10},{14,12},{16,14},{18,16},{20... | collective-permute-start | bytes 1769480 | tf_op jit(solution)/shard_map/ppermute | solution.py:25
  148.0 5.2 %collective-permute-start.13 = (f32[4,2,3,3,2,1,1,128]{7,6,4,3,1,2,5,0:T(1,128)S(1)}, f32[4,2,3,3,2,1,1,128]{7,6,4,3,1,2,5,0:T(1,128)S(1)}, u32[]{:S(2)}, u32[]{:S(2)}) collective-permute-start(f32[4,2,3,3,2,1,1,128]{7,6,4,3,1,2,5,0:T(1,128)S(1)} %get-tuple-element.560), channel_id=1, source_target_pairs={{0,1},{1,0},{2,3},{3,2},{4,5},{5,4},{6,7},{7,6},{8,9},{9,8},{10,11... | collective-permute-start | bytes 221192 | tf_op jit(solution)/shard_map/ppermute | solution.py:24
  151.2 3.2 %collective-permute-start.16 = (f32[4,2,3,3,2,1,1,128]{7,6,4,3,1,2,5,0:T(1,128)S(1)}, f32[4,2,3,3,2,1,1,128]{7,6,4,3,1,2,5,0:T(1,128)S(1)}, u32[]{:S(2)}, u32[]{:S(2)}) collective-permute-start(f32[4,2,3,3,2,1,1,128]{7,6,4,3,1,2,5,0:T(1,128)S(1)} %get-tuple-element.561), channel_id=1, source_target_pairs={{1,0},{0,1},{3,2},{2,3},{5,4},{4,5},{7,6},{6,7},{9,8},{8,9},{11,10... | collective-permute-start | bytes 221192 | tf_op jit(solution)/shard_map/ppermute | solution.py:25
  163.1 22.8 %all-to-all-start = ((f32[8,1,2,3,3,1,8,128]{7,6,4,3,2,5,1,0:T(8,128)}), f32[8,1,2,3,3,1,8,128]{7,6,4,3,2,5,1,0:T(8,128)S(1)}, u32[]{:S(2)}, u32[]{:S(2)}) async-start(f32[8,1,2,3,3,1,8,128]{7,6,4,3,2,5,1,0:T(8,128)} %broadcast_in_dim.4), calls=%async_computation | async-start | bytes 1179648 | tf_op jit(solution)/shard_map/all_to_all | solution.py:65
where the time goes:
time: 210 us; the launch traced here: 209 us
  starting transfers between devices  101 us (48%)
  waiting for transfers between devices  58.8 us (28%)
  blocking collectives  21.4 us (10%)
  other arithmetic  16.7 us (8%)
  local copies, waits for them, and re-layouts  8.01 us (4%)
  between operations  3.02 us (1%)
    ppermute x6, starting transfers between devices, padded_2(): lax.ppermute(head, axis, [((i + 1) % count, i) for i in range(count)])  56.7 us
    ppermute x6, waiting for transfers between devices, padded_2(): lax.ppermute(tail, axis, [(i, (i + 1) % count) for i in range(count)])  23.7 us
    all_to_all x1, blocking collectives, sent_to_all(): return lax.all_to_all(copies, axis, split_axis=0, concat_axis=0, tiled=True)  21.4 us
    ppermute x6, starting transfers between devices, padded_2(): lax.ppermute(tail, axis, [(i, (i + 1) % count) for i in range(count)])  20.7 us
    all_to_all x1, waiting for transfers between devices, sent_to_all(): return lax.all_to_all(copies, axis, split_axis=0, concat_axis=0, tiled=True)  17.2 us
    ppermute x2, starting transfers between devices, with_halo(): lax.ppermute(initial, axis, [(b, a) for a, b in up])  7.3 us
    ppermute x1, waiting for transfers between devices, shifted(): lax.ppermute(shard, axis, [(i, (i + by) % devices) for i in range(devices)])  5.91 us
    ppermute x6, waiting for transfers between devices, padded_2(): lax.ppermute(head, axis, [((i + 1) % count, i) for i in range(count)])  5.73 us
  transfers between devices with their start and end apart: 18, of which 13 were waited for; matrix products, arithmetic and copies ran while one was open for 1% of the time, Pallas kernels for 0%

commit v1 on v0

v1 whole, which is shorter than its diff:
```python
import functools

import jax
import jax.numpy as jnp
from jax import lax
from jax.experimental import pallas as pl
from jax.experimental.pallas import tpu as pltpu
from jax.sharding import PartitionSpec as P

MESH = pl.DeviceIdType.MESH
F32 = jnp.float32
STEPS = 3
FLOOR = 0.25
FX, FY, FZ, FV = 0, 1, 2, 3


def third_row(m):
    (a_re, b_re), (a_im, b_im) = m[0][:2], m[1][:2]
    re, im = [], []
    for k in range(3):
        p, q = (k + 1) % 3, (k + 2) % 3
        re.append(
            a_re[p] * b_re[q] - a_im[p] * b_im[q] - (a_re[q] * b_re[p] - a_im[q] * b_im[p])
        )
        im.append(
            (a_re[q] * b_im[p] + a_im[q] * b_re[p]) - (a_re[p] * b_im[q] + a_im[p] * b_re[q])
        )
    return [m[0][0], m[0][1], re], [m[1][0], m[1][1], im]


def load(ref, lead, rows, count=3):
    return tuple(
        [[ref[(*lead, part, i, j, rows)] for j in range(3)] for i in range(count)]
        for part in range(2)
    )


def load2(ref, lead, rows):
    return third_row(load(ref, lead, rows, 2))


def store(ref, lead, rows, m):
    for part in range(2):
        for i, row in enumerate(m[part]):
            for j, v in enumerate(row):
                ref[(*lead, part, i, j, rows)] = v


def mapped(fn, *ms):
    return tuple(
        [[fn(*vs) for vs in zip(*rows)] for rows in zip(*[m[part] for m in ms])]
        for part in range(2)
    )


def add(*ms):
    return mapped(lambda *vs: functools.reduce(lambda a, b: a + b, vs), *ms)


def ahead_x(m):
    return mapped(lambda v: pltpu.roll(v, v.shape[-1] - 1, 1), m)


def back_x(m):
    return mapped(lambda v: pltpu.roll(v, 1, 1), m)


def mul(a, b, da=False, db=False, rows=3):
    out_re, out_im = [], []
    for i in range(rows):
        row_re, row_im = [], []
        for k in range(3):
            re = im = None
            for j in range(3):
                ar, ai = (a[0][j][i], a[1][j][i]) if da else (a[0][i][j], a[1][i][j])
                br, bi = (b[0][k][j], b[1][k][j]) if db else (b[0][j][k], b[1][j][k])
                rr, ii, ri, ir = ar * br, ai * bi, ar * bi, ai * br
                tr = rr + ii if da != db else rr - ii
                if da and db:
                    ti = -(ri + ir)
                elif da:
                    ti = ri - ir
                elif db:
                    ti = ir - ri
                else:
                    ti = ri + ir
                re = tr if re is None else re + tr
                im = ti if im is None else im + ti
            row_re.append(re)
            row_im.append(im)
        out_re.append(row_re)
        out_im.append(row_im)
    return out_re, out_im


def normalized(re, im):
    weight = sum(v * v for v in re) + sum(v * v for v in im)
    scale = lax.rsqrt(jnp.maximum(weight, FLOOR))
    return [v * scale for v in re], [v * scale for v in im]


def project(re, im):
    u_re, u_im = normalized(re[0], im[0])
    in_re = sum(u_re[j] * re[1][j] + u_im[j] * im[1][j] for j in range(3))
    in_im = sum(u_re[j] * im[1][j] - u_im[j] * re[1][j] for j in range(3))
    w_re = [re[1][j] - (in_re * u_re[j] - in_im * u_im[j]) for j in range(3)]
    w_im = [im[1][j] - (in_re * u_im[j] + in_im * u_re[j]) for j in range(3)]
    v_re, v_im = normalized(w_re, w_im)
    return third_row(([u_re, v_re], [u_im, v_im]))


def mixed(link, staples, weight):
    re = [[0.5 * link[0][i][j] + weight * staples[0][i][j] for j in range(3)] for i in range(2)]
    im = [[0.5 * link[1][i][j] + weight * staples[1][i][j] for j in range(3)] for i in range(2)]
    return project(re, im)


def kernel(
    ta, gz, half,
    sp, tl, pol, mean,
    F, T, H, TH, UP, S, L, AB, M, sm, ar, tree, pb, bc, zs,
    local_sem, send_sem, recv_sem, out_sem,
):
    j, z, h = lax.axis_index("ta"), lax.axis_index("gz"), lax.axis_index("gy")
    o = 1 - h
    zp, zm = lax.rem(z + 1, gz), lax.rem(z + gz - 1, gz)
    full = 2 * half
    nd = 2 * ta
    own = full // nd
    me = 2 * j + h
    mine = pl.ds(pl.multiple_of(h * half, half), half)
    halves = [pl.ds(k * half, half) for k in range(2)]

    sent = []
    n_sem = [0, 0]

    def remote(src, dst, recv_index, **where):
        k = n_sem[0]
        n_sem[0] += 1
        copy = pltpu.make_async_remote_copy(
            src_ref=src, dst_ref=dst, send_sem=send_sem.at[k], recv_sem=recv_sem.at[recv_index],
            device_id=where, device_id_type=MESH,
        )
        copy.start()
        sent.append(copy)

    def arrived(dst, recv_index):
        pltpu.make_async_remote_copy(
            src_ref=dst, dst_ref=dst, send_sem=send_sem.at[0], recv_sem=recv_sem.at[recv_index],
            device_id={"gy": o}, device_id_type=MESH,
        ).wait_recv()

    def new_recv(n=1):
        k = n_sem[1]
        n_sem[1] += n
        return k

    near = [
        pltpu.make_async_copy(sp.at[:, :, :, :, h, 0], F.at[0, 0:3, :, :, :, mine], local_sem.at[0]),
        pltpu.make_async_copy(tl.at[:, :, :, h, 0], T.at[:, :, :, mine], local_sem.at[1]),
    ]
    for copy in near:
        copy.start()

    barrier = pltpu.get_barrier_semaphore()
    count = 0
    for k in range(1, nd):
        d = lax.rem(me + k, nd)
        pl.semaphore_signal(
            barrier, inc=1, device_id={"ta": d // 2, "gy": lax.rem(d, 2)}, device_id_type=MESH
        )
        count += 1
    for k in range(1, gz):
        pl.semaphore_signal(
            barrier, inc=1, device_id={"gz": lax.rem(z + k, gz)}, device_id_type=MESH
        )
        count += 1
    for k in sorted({1 % gz, (gz - 1) % gz}):
        pl.semaphore_signal(
            barrier, inc=1, device_id={"gz": lax.rem(z + k, gz), "gy": o}, device_id_type=MESH
        )
        count += 1
    pl.semaphore_wait(barrier, count)

    r_v, r_x, r_y, r_t = new_recv(2), new_recv(4), new_recv(4), new_recv(4)
    r_own, r_ownt = new_recv(), new_recv()

    def plane(f, t):
        return sp.at[f, :, 0:2, :, t, 0] if f is not None else tl.at[:, 0:2, :, t, 0]

    def two(ref, *lead):
        return ref.at[(*lead, slice(None), slice(0, 2), slice(None), mine)]

    for t in range(2):
        remote(plane(FZ, t), two(F, 0, FV), r_v + h, gz=zp, gy=t)
    remote(sp.at[:, :, :, :, o, 0], F.at[0, 0:3, :, :, :, mine], r_own, gy=o)
    for f, r in ((FX, r_x), (FY, r_y)):
        for t in range(2):
            remote(plane(f, t), two(H, 0, 0, f), r + h, gz=zm, gy=t)
            remote(plane(f, t), two(H, 0, 1, f), r + 2 + h, gz=zp, gy=t)
    remote(tl.at[:, :, :, o, 0], T.at[:, :, :, mine], r_ownt, gy=o)
    for t in range(2):
        remote(plane(None, t), two(TH, 0), r_t + h, gz=zm, gy=t)
        remote(plane(None, t), two(TH, 1), r_t + 2 + h, gz=zp, gy=t)

    def each_half(body):
        def run(k, carry):
            r0 = pl.multiple_of(k * half, half)
            body(pl.ds(r0, half), pl.ds(r0 + 1, half))
            return carry

        lax.fori_loop(0, 2, run, 0)

    def wrap(ref, *lead):
        ref[(*lead, slice(None), slice(None), slice(None), pl.ds(full, 1))] = ref[
            (*lead, slice(None), slice(None), slice(None), pl.ds(0, 1))
        ]

    def unwrap(k):
        L[k, :, :, :, pl.ds(0, 1)] = L[k, :, :, :, pl.ds(full, 1)]

    def in_plane(s):
        def body(rows, up):
            ux, uy = load(F, (s, FX), rows), load(F, (s, FY), rows)
            uy_x, ux_y = ahead_x(uy), load(F, (s, FX), up)
            c, d = mul(ux, uy_x), mul(uy, ux_y)
            store(S, (FX,), rows, mul(d, uy_x, db=True, rows=2))
            store(L, (0,), up, mul(uy, c, da=True, rows=2))
            store(
                S, (FY,), rows,
                add(mul(c, ux_y, db=True, rows=2), back_x(mul(ux, d, da=True, rows=2))),
            )

        each_half(body)
        unwrap(0)

    def side(ref, s, f, rows, up):
        return ahead_x(load(ref, (s, f), rows)) if up is None else load(ref, (s, f), up)

    def across(s, f):
        def body(rows, up):
            up = None if f == FX else up
            uz, uz_f = load(F, (s, FZ), rows), side(F, s, FZ, rows, up)
            a = mul(uz, load2(H, (s, 0, f), rows))
            store(AB, (0,), rows, a)
            total = add(load(S, (f,), rows, 2), mul(a, uz_f, db=True, rows=2))
            uv, uv_f = load(F, (s, FV), rows), side(F, s, FV, rows, up)
            b = mul(load2(H, (s, 1, f), rows), uv_f)
            store(AB, (1,), rows, b)
            total = add(total, mul(uv, b, da=True, rows=2))
            if f == FX:
                total = add(total, load(L, (0,), rows, 2))
            store(F, (s + 1, f), rows, mixed(load(F, (s, f), rows, 2), total, 0.125))

        each_half(body)

    def z_staples(s, f):
        def body(rows, up):
            shift = None if f == FX else up
            uf = load(F, (s, f), rows)
            b = mul(uf, side(F, s, FZ, rows, shift), rows=2)
            upper = mul(b, load2(H, (s, 0, f), rows), db=True, rows=2)
            lower = mul(uf, load(AB, (0,), rows), da=True, rows=2)
            below = load2(H, (s, 1, f), rows)
            v_upper = mul(load(AB, (1,), rows), uf, db=True, rows=2)
            v_lower = mul(mul(below, load(F, (s, FV), rows), da=True, rows=2), uf, rows=2)
            if f == FX:
                store(S, (FZ,), rows, add(upper, back_x(lower)))
                store(S, (FV,), rows, add(v_upper, back_x(v_lower)))
            else:
                store(L, (1,), up, lower)
                store(L, (2,), up, v_lower)
                store(S, (FZ,), rows, add(load(S, (FZ,), rows, 2), upper))
                store(S, (FV,), rows, add(load(S, (FV,), rows, 2), v_upper))

        each_half(body)
        if f == FY:
            unwrap(1)
            unwrap(2)

    def z_links(s):
        def body(rows, up):
            for f, k in ((FZ, 1), (FV, 2)):
                total = add(load(S, (f,), rows, 2), load(L, (k,), rows, 2))
                store(F, (s + 1, f), rows, mixed(load(F, (s, f), rows, 2), total, 0.125))

        each_half(body)
        wrap(F, s + 1, FZ)
        wrap(F, s + 1, FV)

    for copy in near:
        copy.wait()
    other = pl.ds(pl.multiple_of(o * half, half), half)
    arrived(F.at[0, 0:3, :, :, :, other], r_own)
    wrap(F, 0, FX)
    wrap(F, 0, FZ)
    in_plane(0)
    for k in range(2):
        arrived(F.at[0, FV, :, 0:2, :, halves[k]], r_v + k)

    def complete(rows, up):
        store(F, (0, FV), rows, load2(F, (0, FV), rows))

    each_half(complete)
    wrap(F, 0, FV)

    r_next = new_recv(4)

    def onward(s, f):
        remote(
            F.at[s, f, :, 0:2, :, 0:full], UP.at[f], r_next + f,
            ta=lax.rem(j + h + ta - 1, ta), gy=o,
        )

    for s in range(STEPS):
        last = s == STEPS - 1
        sems = {}
        for f in (FX, FY):
            if s == 0:
                for side_k in range(2):
                    for k in range(2):
                        arrived(
                            H.at[0, side_k, f, :, :, :, halves[k]],
                            (r_x, r_y)[f] + 2 * side_k + k,
                        )
            else:
                for side_k in range(2):
                    arrived(H.at[s, side_k, f], r_now[f] + side_k)
            across(s, f)
            if f == FX:
                wrap(F, s + 1, FX)
            if last:
                onward(s + 1, f)
            else:
                sems[f] = new_recv(2)
                out = F.at[s + 1, f, :, 0:2, :, 0:full]
                remote(out, H.at[s + 1, 0, f], sems[f], gz=zm)
                remote(out, H.at[s + 1, 1, f], sems[f] + 1, gz=zp)
            z_staples(s, f)
        r_now = sems
        z_links(s)
        if last:
            onward(s + 1, FZ)
            onward(s + 1, FV)
        else:
            in_plane(s + 1)

    n = STEPS
    arrived(T.at[:, :, :, other], r_ownt)
    wrap(T)
    for side_k in range(2):
        for k in range(2):
            arrived(TH.at[side_k, :, :, :, halves[k]], r_t + 2 * side_k + k)

    def before(rows, up):
        t = load(T, (), rows)
        ux, uy = load(F, (n, FX), rows), load(F, (n, FY), rows)
        store(M, (0,), rows, mul(ux, ahead_x(t), rows=2))
        store(M, (1,), rows, mul(ux, t, da=True, rows=2))
        store(M, (2,), rows, mul(uy, load(T, (), up), rows=2))
        store(M, (3,), rows, mul(uy, t, da=True, rows=2))
        store(M, (4,), rows, mul(load(F, (n, FZ), rows), load2(TH, (0,), rows), rows=2))
        store(
            M, (5,), rows, mul(load(F, (n, FV), rows), load2(TH, (1,), rows), da=True, rows=2)
        )

    each_half(before)
    arrived(UP.at[FX], r_next + FX)
    arrived(UP.at[FY], r_next + FY)

    def along_xy(rows, up):
        ux, uy = load2(UP, (FX,), rows), load2(UP, (FY,), rows)
        total = add(
            mul(load(M, (0,), rows, 2), ux, db=True, rows=2),
            back_x(mul(load(M, (1,), rows, 2), ux, rows=2)),
            mul(load(M, (2,), rows, 2), uy, db=True, rows=2),
        )
        store(S, (0,), rows, total)
        store(L, (0,), up, mul(load(M, (3,), rows, 2), uy, rows=2))

    each_half(along_xy)
    unwrap(0)
    arrived(UP.at[FZ], r_next + FZ)
    arrived(UP.at[FV], r_next + FV)

    def finish(k, carry):
        r0 = pl.multiple_of(k * half, half)
        rows = pl.ds(r0, half)
        uz, uv = load2(UP, (FZ,), rows), load2(UP, (FV,), rows)
        total = add(
            load(S, (0,), rows, 2),
            load(L, (0,), rows, 2),
            mul(load(M, (4,), rows, 2), uz, db=True, rows=2),
            mul(load(M, (5,), rows, 2), uv, rows=2),
        )
        done = mixed(load(T, (), rows, 2), total, 0.5 / 6.0)
        for part in range(2):
            for a in range(2):
                for b in range(3):
                    sm[pl.ds(r0 * 16 + part * 6 + a * 3 + b, half, 16), :] = done[part][a][b]
        return carry

    lax.fori_loop(0, 2, finish, 0)

    span = own * 16
    r_row = new_recv(nd)
    here = pl.ds(pl.multiple_of(me * span, 8), span)
    for k in range(1, nd):
        d = lax.rem(me + k, nd)
        remote(
            sm.at[pl.ds(pl.multiple_of(d * span, 8), span)], ar.at[here], r_row + me,
            ta=d // 2, gy=lax.rem(d, 2),
        )
    ar[here, :] = sm[here, :]
    for k in range(1, nd):
        d = lax.rem(me + k, nd)
        arrived(ar.at[pl.ds(pl.multiple_of(d * span, 8), span)], r_row + d)

    def slices(start, stride, rows):
        at = lambda c: ar[pl.ds(start + c, rows, stride), :]
        return third_row(
            tuple([[at(part * 6 + a * 3 + b) for b in range(3)] for a in range(2)] for part in range(2))
        )

    for row in range(own):
        rows = nd // 2
        lhs, rhs = slices(row * 16, 2 * span, rows), slices(row * 16 + span, 2 * span, rows)
        while rows > 1:
            prod = mul(lhs, rhs)
            flat = [v for part in prod for line in part for v in line]
            for c, v in enumerate(flat):
                tree[pl.ds(c * 8, rows), :] = v
            rows //= 2
            pick = lambda first: [tree[pl.ds(c * 8 + first, rows, 2), :] for c in range(18)]
            grid = lambda vs: tuple(
                [[vs[part * 9 + a * 3 + b] for b in range(3)] for a in range(3)] for part in range(2)
            )
            lhs, rhs = grid(pick(0)), grid(pick(1))
        re = im = None
        for a in range(3):
            for b in range(3):
                lr, li, rr, ri = lhs[0][a][b], lhs[1][a][b], rhs[0][b][a], rhs[1][b][a]
                t_re, t_im = lr * rr - li * ri, lr * ri + li * rr
                re = t_re if re is None else re + t_re
                im = t_im if im is None else im + t_im
        pb[row, 0:1, :] = re / 3.0
        pb[row, 1:2, :] = im / 3.0

    r_out = new_recv(nd)
    home = pl.ds(me * own, own)
    for k in range(1, nd):
        d = lax.rem(me + k, nd)
        remote(pb, bc.at[home], r_out + me, ta=d // 2, gy=lax.rem(d, 2))
    bc[home] = pb[...]
    for k in range(1, nd):
        d = lax.rem(me + k, nd)
        arrived(bc.at[pl.ds(d * own, own)], r_out + d)

    sums = jnp.sum(bc[...], axis=0)
    zs[z] = sums
    r_sum = new_recv(gz)
    for k in range(1, gz):
        remote(zs.at[z], zs.at[z], r_sum + z, gz=lax.rem(z + k, gz))
    for k in range(half):
        pol[:, 0, k, :] = bc[h * half + k]
    for k in range(1, gz):
        d = lax.rem(z + k, gz)
        arrived(zs.at[d], r_sum + d)
    totals = jnp.sum(zs[...], axis=0)
    sites = float(full * gz * sp.shape[-1])
    for part in range(2):
        mean[part] = jnp.sum(totals[part : part + 1, :]) / sites

    for copy in sent:
        copy.wait_send()


def solution(mesh):
    ta, gz = mesh.shape["ta"], mesh.shape["gz"]

    def body(sp, tl):
        half, lanes = sp.shape[-2:]
        full = 2 * half
        pad = full + 8
        nd = 2 * ta
        own = full // nd

        def vmem(*dims):
            return pltpu.VMEM((*dims, lanes), F32)

        n_send = 2 + 1 + 8 + 1 + 4 + 4 * (STEPS - 1) + 4 + 2 * (nd - 1) + gz - 1
        n_recv = 2 + 4 + 4 + 4 + 2 + 4 + 4 * (STEPS - 1) + 2 * nd + gz
        return pl.pallas_call(
            functools.partial(kernel, ta, gz, half),
            out_shape=(
                jax.ShapeDtypeStruct((2, 1, half, lanes), F32),
                jax.ShapeDtypeStruct((2,), F32),
            ),
            in_specs=[pl.BlockSpec(memory_space=pl.ANY)] * 2,
            out_specs=(
                pl.BlockSpec(memory_space=pltpu.VMEM),
                pl.BlockSpec(memory_space=pltpu.SMEM),
            ),
            scratch_shapes=[
                vmem(STEPS + 1, 4, 2, 3, 3, pad),
                vmem(2, 3, 3, pad),
                vmem(STEPS, 2, 2, 2, 2, 3, full),
                vmem(2, 2, 2, 3, full),
                vmem(4, 2, 2, 3, full),
                vmem(4, 2, 2, 3, full),
                vmem(3, 2, 2, 3, pad),
                vmem(2, 2, 3, 3, full),
                vmem(6, 2, 2, 3, full),
                vmem(full * 16),
                vmem(full * 16),
                vmem(18 * 8),
                vmem(own, 2),
                vmem(full, 2),
                vmem(gz, 2),
                pltpu.SemaphoreType.DMA((2,)),
                pltpu.SemaphoreType.DMA((n_send,)),
                pltpu.SemaphoreType.DMA((n_recv,)),
                pltpu.SemaphoreType.DMA,
            ],
            compiler_params=pltpu.CompilerParams(
                collective_id=0, has_side_effects=True, vmem_limit_bytes=32 * 1024 * 1024
            ),
        )(sp, tl)

    return jax.shard_map(
        body,
        mesh=mesh,
        in_specs=(
            P("cfg", None, None, None, "ta", "gz", "gy", None),
            P("cfg", None, None, "ta", "gz", "gy", None),
        ),
        out_specs=(P("cfg", "gz", "gy", None), P("cfg")),
        check_vma=False,
    )
```

time: 210 us -> 97.9 us (0.47)
  starting transfers between devices: 101 us -> 0 us
  Pallas kernels: 0 us -> 94.1 us
  waiting for transfers between devices: 58.8 us -> 0 us
  blocking collectives: 21.4 us -> 0 us
  other arithmetic: 16.7 us -> 0 us
  local copies, waits for them, and re-layouts: 8.01 us -> 3.03 us
  between operations: 3.02 us -> 0.65 us
    ppermute x17 -> x0, starting transfers between devices: 95.3 us -> none  [the longest x6 56.7 us: padded_2(): lax.ppermute(head, axis, [((i + 1) % count, i) for i in range(count)])]
    pallas_call x0 -> x1, Pallas kernels: none -> 94.1 us  [body(): pl.pallas_call(functools.partial(kernel, ta, gz, half), out_shape=(jax.Sh...]
    ppermute x17 -> x0, waiting for transfers between devices: 41.7 us -> none  [the longest x6 23.7 us: padded_2(): lax.ppermute(tail, axis, [(i, (i + 1) % count) for i in range(count)])]
    all_to_all x1 -> x0, blocking collectives: 21.4 us -> none  [sent_to_all(): return lax.all_to_all(copies, axis, split_axis=0, concat_axis=0, tiled=True)]
    all_to_all x1 -> x0, waiting for transfers between devices: 17.2 us -> none  [sent_to_all(): return lax.all_to_all(copies, axis, split_axis=0, concat_axis=0, tiled=True)]
    reduce_sum x104 -> x0, other arithmetic: 6.61 us -> none  [the longest x72 5.57 us: mat_product(): real_part = jnp.sum(lhs_re * rhs_re - lhs_im * rhs_im, axis=1)]
    all_to_all x1 -> x0, starting transfers between devices: 5.7 us -> none  [sent_to_all(): return lax.all_to_all(copies, axis, split_axis=0, concat_axis=0, tiled=True)]
    mul x41 -> x0, other arithmetic: 3.8 us -> none  [mat_product(): real_part = jnp.sum(lhs_re * rhs_re - lhs_im * rhs_im, axis=1)]
  transfers between devices with their start and end apart: 18 -> 0, of which waited for: 13 -> 0; matrix products, arithmetic and copies ran while one was open for 1% -> 0% of each run, Pallas kernels for 0% -> 0%
where the time goes in v1:
time: 97.9 us; the launch traced here: 97.7 us
  Pallas kernels  94.1 us (96%)
  local copies, waits for them, and re-layouts  3.03 us (3%)
    pallas_call x1, Pallas kernels, body(): pl.pallas_call(functools.partial(kernel, ta, gz, half), out_shape=(jax.Sh...  94.1 us
    unnamed x6, local copies, waits for them, and re-layouts  3.03 us

profile of v1, /device:TPU:65, one launch (start us, length us, event | category | flops | bytes accessed | tf_op | source)
XLA Modules:
  0.0 97.7 jit_solution(10431908237494468669)
XLA Ops:
  0.6 0.0 copy-start
  0.6 1.0 %copy-done = f32[3,2,3,3,2,1,8,128]{7,6,5,4,3,2,1,0:T(8,128)S(1)} copy-done((f32[3,2,3,3,2,1,8,128]{7,6,5,4,3,2,1,0:T(8,128)S(1)}, f32[3,2,3,3,2,1,8,128]{7,6,5,4,3,2,1,0:T(8,128)}, u32[]{:S(2)}) %copy-start) | copy-done | bytes 442392
  1.6 0.0 copy-start.1
  1.6 0.9 copy-done.1
  2.6 94.1 %shard_map.41 = (f32[2,1,8,128]{3,2,1,0:T(8,128)S(1)}, f32[2]{0:T(128)S(1)}) custom-call(f32[3,2,3,3,2,1,8,128]{7,6,5,4,3,2,1,0:T(8,128)S(1)} %copy-done, f32[2,3,3,2,1,8,128]{6,5,4,3,2,1,0:T(8,128)S(1)} %copy-done.1), custom_call_target="tpu_custom_call" | custom-call | tf_op jit(solution)/shard_map/pallas_call | solution.py:493
  96.6 0.6 copy.6
  97.2 0.5 copy.7
Async XLA Ops:
  0.6 1.0 %copy-start = (f32[3,2,3,3,2,1,8,128]{7,6,5,4,3,2,1,0:T(8,128)S(1)}, f32[3,2,3,3,2,1,8,128]{7,6,5,4,3,2,1,0:T(8,128)}, u32[]{:S(2)}) copy-start(f32[3,2,3,3,2,1,8,128]{7,6,5,4,3,2,1,0:T(8,128)} %sp.1) | copy-start | bytes 1327108
  1.6 0.9 copy-start.1

commit v2 on v1

--- a/solution.py
+++ b/solution.py
@@ -119,7 +119,7 @@
     ta, gz, half,
     sp, tl, pol, mean,
     F, T, H, TH, UP, S, L, AB, M, sm, ar, tree, pb, bc, zs,
-    local_sem, send_sem, recv_sem, out_sem,
+    local_sem, send_sem, recv_sem, ready_sem,
 ):
     j, z, h = lax.axis_index("ta"), lax.axis_index("gz"), lax.axis_index("gy")
     o = 1 - h
@@ -163,24 +163,31 @@
         copy.start()
 
     barrier = pltpu.get_barrier_semaphore()
-    count = 0
-    for k in range(1, nd):
-        d = lax.rem(me + k, nd)
-        pl.semaphore_signal(
-            barrier, inc=1, device_id={"ta": d // 2, "gy": lax.rem(d, 2)}, device_id_type=MESH
-        )
-        count += 1
-    for k in range(1, gz):
-        pl.semaphore_signal(
-            barrier, inc=1, device_id={"gz": lax.rem(z + k, gz)}, device_id_type=MESH
-        )
-        count += 1
-    for k in sorted({1 % gz, (gz - 1) % gz}):
-        pl.semaphore_signal(
-            barrier, inc=1, device_id={"gz": lax.rem(z + k, gz), "gy": o}, device_id_type=MESH
-        )
-        count += 1
-    pl.semaphore_wait(barrier, count)
+    around = sorted({(0, 1 % gz), (0, (gz - 1) % gz), (1 % ta, 0), ((ta - 1) % ta, 0)} - {(0, 0)})
+
+    def place(dx, dz):
+        return {"ta": lax.rem(j + dx, ta), "gz": lax.rem(z + dz, gz)}
+
+    def signal(sem, **where):
+        pl.semaphore_signal(sem, inc=1, device_id=where, device_id_type=MESH)
+
+    signal(barrier, gy=o)
+    for dx, dz in around:
+        for c in range(2):
+            signal(barrier, **place(dx, dz), gy=c)
+    pl.semaphore_wait(barrier, 1 + 2 * len(around))
+
+    rounds = max(ta // 2, gz // 2) - 1
+    heard = [0]
+
+    def hear(count=1):
+        for _ in range(count):
+            if 0 < heard[0] <= rounds:
+                pl.semaphore_wait(ready_sem.at[heard[0] - 1], len(around))
+            heard[0] += 1
+            if heard[0] <= rounds:
+                for dx, dz in around:
+                    signal(ready_sem.at[heard[0] - 1], **place(dx, dz))
 
     r_v, r_x, r_y, r_t = new_recv(2), new_recv(4), new_recv(4), new_recv(4)
     r_own, r_ownt = new_recv(), new_recv()
@@ -201,7 +208,7 @@
     remote(tl.at[:, :, :, o, 0], T.at[:, :, :, mine], r_ownt, gy=o)
     for t in range(2):
         remote(plane(None, t), two(TH, 0), r_t + h, gz=zm, gy=t)
-        remote(plane(None, t), two(TH, 1), r_t + 2 + h, gz=zp, gy=t)
+    hear()
 
     def each_half(body):
         def run(k, carry):
@@ -295,6 +302,7 @@
     wrap(F, 0, FX)
     wrap(F, 0, FZ)
     in_plane(0)
+    hear()
     for k in range(2):
         arrived(F.at[0, FV, :, 0:2, :, halves[k]], r_v + k)
 
@@ -336,14 +344,21 @@
                 out = F.at[s + 1, f, :, 0:2, :, 0:full]
                 remote(out, H.at[s + 1, 0, f], sems[f], gz=zm)
                 remote(out, H.at[s + 1, 1, f], sems[f] + 1, gz=zp)
+            hear()
             z_staples(s, f)
         r_now = sems
+        if s == STEPS - 2:
+            for t in range(2):
+                remote(plane(None, t), two(TH, 1), r_t + 2 + h, gz=zp, gy=t)
         z_links(s)
         if last:
             onward(s + 1, FZ)
             onward(s + 1, FV)
         else:
+            hear()
             in_plane(s + 1)
+    while heard[0] <= rounds:
+        hear()
 
     n = STEPS
     arrived(T.at[:, :, :, other], r_ownt)
@@ -404,9 +419,10 @@
 
     span = own * 16
     r_row = new_recv(nd)
+    offsets = sorted(range(1, nd), key=lambda k: -min(k // 2, ta - k // 2))
     here = pl.ds(pl.multiple_of(me * span, 8), span)
-    for k in range(1, nd):
-        d = lax.rem(me + k, nd)
+    for k in offsets:
+        d = 2 * lax.rem(j + k // 2, ta) + lax.rem(h + k, 2)
         remote(
             sm.at[pl.ds(pl.multiple_of(d * span, 8), span)], ar.at[here], r_row + me,
             ta=d // 2, gy=lax.rem(d, 2),
@@ -448,8 +464,8 @@
 
     r_out = new_recv(nd)
     home = pl.ds(me * own, own)
-    for k in range(1, nd):
-        d = lax.rem(me + k, nd)
+    for k in offsets:
+        d = 2 * lax.rem(j + k // 2, ta) + lax.rem(h + k, 2)
         remote(pb, bc.at[home], r_out + me, ta=d // 2, gy=lax.rem(d, 2))
     bc[home] = pb[...]
     for k in range(1, nd):
@@ -459,7 +475,7 @@
     sums = jnp.sum(bc[...], axis=0)
     zs[z] = sums
     r_sum = new_recv(gz)
-    for k in range(1, gz):
+    for k in sorted(range(1, gz), key=lambda k: -min(k, gz - k)):
         remote(zs.at[z], zs.at[z], r_sum + z, gz=lax.rem(z + k, gz))
     for k in range(half):
         pol[:, 0, k, :] = bc[h * half + k]
@@ -520,10 +536,10 @@
                 pltpu.SemaphoreType.DMA((2,)),
                 pltpu.SemaphoreType.DMA((n_send,)),
                 pltpu.SemaphoreType.DMA((n_recv,)),
-                pltpu.SemaphoreType.DMA,
+                pltpu.SemaphoreType.REGULAR((max(ta // 2, gz // 2),)),
             ],
             compiler_params=pltpu.CompilerParams(
-                collective_id=0, has_side_effects=True, vmem_limit_bytes=32 * 1024 * 1024
+                collective_id=0, has_side_effects=True, vmem_limit_bytes=63 * 1024 * 1024
             ),
         )(sp, tl)
 

time: 97.9 us -> 88.8 us (0.907)
  Pallas kernels: 94.1 us -> 86.1 us
  local copies, waits for them, and re-layouts: 3.03 us -> 1.81 us
    pallas_call x1, Pallas kernels: 94.1 us -> 86.1 us  [body(): pl.pallas_call(functools.partial(kernel, ta, gz, half), out_shape=(jax.Sh...]
    unnamed x6 -> x4, local copies, waits for them, and re-layouts: 3.03 us -> 1.81 us
where the time goes in v2:
time: 88.8 us; the launch traced here: 88.6 us
  Pallas kernels  86.1 us (97%)
  local copies, waits for them, and re-layouts  1.81 us (2%)
    pallas_call x1, Pallas kernels, body(): pl.pallas_call(functools.partial(kernel, ta, gz, half), out_shape=(jax.Sh...  86.1 us
    unnamed x4, local copies, waits for them, and re-layouts  1.81 us

profile of v2, /device:TPU:65, one launch (start us, length us, event | category | flops | bytes accessed | tf_op | source)
XLA Modules:
  0.0 88.6 jit_solution(9227592392083481682)
XLA Ops:
  0.6 86.1 %shard_map.41 = (f32[2,1,8,128]{3,2,1,0:T(8,128)}, f32[2]{0:T(128)}) custom-call(f32[3,2,3,3,2,1,8,128]{7,6,5,4,3,2,1,0:T(8,128)} %sp.1, f32[2,3,3,2,1,8,128]{6,5,4,3,2,1,0:T(8,128)} %tl.1), custom_call_target="tpu_custom_call" | custom-call | tf_op jit(solution)/shard_map/pallas_call | solution.py:509
  86.8 0.0 copy-start
  86.8 1.3 %copy.6 = f32[2,1,8,128]{3,2,1,0:T(8,128)} copy(f32[2,1,8,128]{3,2,1,0:T(8,128)} %get-tuple-element.4) | data formatting | bytes 16384
  88.1 0.0 copy-done
  88.1 0.5 copy.7
Async XLA Ops:
  86.8 1.3 %copy-start = (f32[2]{0:T(128)S(1)}, f32[2]{0:T(128)}, u32[]{:S(2)}) copy-start(f32[2]{0:T(128)} %get-tuple-element.5) | copy-start | bytes 28

commit v3 on v2

--- a/solution.py
+++ b/solution.py
@@ -119,11 +119,14 @@
     ta, gz, half,
     sp, tl, pol, mean,
     F, T, H, TH, UP, S, L, AB, M, sm, ar, tree, pb, bc, zs,
-    local_sem, send_sem, recv_sem, ready_sem,
+    local_sem, send_sem, recv_sem, ready_x, ready_z,
 ):
+    def wrapped(v, n):
+        return jnp.where(v >= n, v - n, v)
+
     j, z, h = lax.axis_index("ta"), lax.axis_index("gz"), lax.axis_index("gy")
     o = 1 - h
-    zp, zm = lax.rem(z + 1, gz), lax.rem(z + gz - 1, gz)
+    zp, zm = wrapped(z + 1, gz), wrapped(z + gz - 1, gz)
     full = 2 * half
     nd = 2 * ta
     own = full // nd
@@ -166,7 +169,7 @@
     around = sorted({(0, 1 % gz), (0, (gz - 1) % gz), (1 % ta, 0), ((ta - 1) % ta, 0)} - {(0, 0)})
 
     def place(dx, dz):
-        return {"ta": lax.rem(j + dx, ta), "gz": lax.rem(z + dz, gz)}
+        return {"ta": wrapped(j + dx, ta), "gz": wrapped(z + dz, gz)}
 
     def signal(sem, **where):
         pl.semaphore_signal(sem, inc=1, device_id=where, device_id_type=MESH)
@@ -177,17 +180,28 @@
             signal(barrier, **place(dx, dz), gy=c)
     pl.semaphore_wait(barrier, 1 + 2 * len(around))
 
-    rounds = max(ta // 2, gz // 2) - 1
-    heard = [0]
-
-    def hear(count=1):
-        for _ in range(count):
-            if 0 < heard[0] <= rounds:
-                pl.semaphore_wait(ready_sem.at[heard[0] - 1], len(around))
-            heard[0] += 1
-            if heard[0] <= rounds:
-                for dx, dz in around:
-                    signal(ready_sem.at[heard[0] - 1], **place(dx, dz))
+    def relay(sem, rounds, sides):
+        done = [0]
+
+        def go(last=False):
+            while True:
+                if 0 < done[0] <= rounds:
+                    pl.semaphore_wait(sem.at[done[0] - 1], len(sides))
+                done[0] += 1
+                if done[0] <= rounds:
+                    for where in sides:
+                        signal(sem.at[done[0] - 1], **where)
+                if not last or done[0] > rounds:
+                    return
+
+        return go
+
+    hear_x = relay(
+        ready_x, ta // 2 - 1, [{"ta": wrapped(j + k, ta)} for k in sorted({1 % ta, ta - 1} - {0})]
+    )
+    hear_z = relay(
+        ready_z, gz // 2 - STEPS, [{"gz": wrapped(z + k, gz)} for k in sorted({1 % gz, gz - 1} - {0})]
+    )
 
     r_v, r_x, r_y, r_t = new_recv(2), new_recv(4), new_recv(4), new_recv(4)
     r_own, r_ownt = new_recv(), new_recv()
@@ -208,7 +222,7 @@
     remote(tl.at[:, :, :, o, 0], T.at[:, :, :, mine], r_ownt, gy=o)
     for t in range(2):
         remote(plane(None, t), two(TH, 0), r_t + h, gz=zm, gy=t)
-    hear()
+    hear_x()
 
     def each_half(body):
         def run(k, carry):
@@ -302,7 +316,6 @@
     wrap(F, 0, FX)
     wrap(F, 0, FZ)
     in_plane(0)
-    hear()
     for k in range(2):
         arrived(F.at[0, FV, :, 0:2, :, halves[k]], r_v + k)
 
@@ -317,7 +330,7 @@
     def onward(s, f):
         remote(
             F.at[s, f, :, 0:2, :, 0:full], UP.at[f], r_next + f,
-            ta=lax.rem(j + h + ta - 1, ta), gy=o,
+            ta=wrapped(j + h + ta - 1, ta), gy=o,
         )
 
     for s in range(STEPS):
@@ -344,7 +357,10 @@
                 out = F.at[s + 1, f, :, 0:2, :, 0:full]
                 remote(out, H.at[s + 1, 0, f], sems[f], gz=zm)
                 remote(out, H.at[s + 1, 1, f], sems[f] + 1, gz=zp)
-            hear()
+            if f == FY:
+                hear_x(last)
+            if last:
+                hear_z()
             z_staples(s, f)
         r_now = sems
         if s == STEPS - 2:
@@ -355,10 +371,7 @@
             onward(s + 1, FZ)
             onward(s + 1, FV)
         else:
-            hear()
             in_plane(s + 1)
-    while heard[0] <= rounds:
-        hear()
 
     n = STEPS
     arrived(T.at[:, :, :, other], r_ownt)
@@ -380,6 +393,7 @@
         )
 
     each_half(before)
+    hear_z()
     arrived(UP.at[FX], r_next + FX)
     arrived(UP.at[FY], r_next + FY)
 
@@ -394,6 +408,7 @@
         store(L, (0,), up, mul(load(M, (3,), rows, 2), uy, rows=2))
 
     each_half(along_xy)
+    hear_z()
     unwrap(0)
     arrived(UP.at[FZ], r_next + FZ)
     arrived(UP.at[FV], r_next + FV)
@@ -418,19 +433,22 @@
     lax.fori_loop(0, 2, finish, 0)
 
     span = own * 16
+    sm3, ar3 = sm.reshape(full, 16, sm.shape[-1]), ar.reshape(full, 16, sm.shape[-1])
     r_row = new_recv(nd)
     offsets = sorted(range(1, nd), key=lambda k: -min(k // 2, ta - k // 2))
-    here = pl.ds(pl.multiple_of(me * span, 8), span)
+    here = pl.ds(me * own, own)
+
+    def part_of(ref, d):
+        return ref.at[pl.ds(d * own, own), 0:12]
+
     for k in offsets:
-        d = 2 * lax.rem(j + k // 2, ta) + lax.rem(h + k, 2)
-        remote(
-            sm.at[pl.ds(pl.multiple_of(d * span, 8), span)], ar.at[here], r_row + me,
-            ta=d // 2, gy=lax.rem(d, 2),
-        )
-    ar[here, :] = sm[here, :]
+        dj, dh = wrapped(j + k // 2, ta), (h if k % 2 == 0 else o)
+        remote(part_of(sm3, 2 * dj + dh), part_of(ar3, me), r_row + me, ta=dj, gy=dh)
+    hear_z()
+    ar3[here] = sm3[here]
     for k in range(1, nd):
-        d = lax.rem(me + k, nd)
-        arrived(ar.at[pl.ds(pl.multiple_of(d * span, 8), span)], r_row + d)
+        d = wrapped(me + k, nd)
+        arrived(part_of(ar3, d), r_row + d)
 
     def slices(start, stride, rows):
         at = lambda c: ar[pl.ds(start + c, rows, stride), :]
@@ -462,30 +480,31 @@
         pb[row, 0:1, :] = re / 3.0
         pb[row, 1:2, :] = im / 3.0
 
+    hear_z(True)
     r_out = new_recv(nd)
     home = pl.ds(me * own, own)
     for k in offsets:
-        d = 2 * lax.rem(j + k // 2, ta) + lax.rem(h + k, 2)
-        remote(pb, bc.at[home], r_out + me, ta=d // 2, gy=lax.rem(d, 2))
+        remote(
+            pb, bc.at[home], r_out + me, ta=wrapped(j + k // 2, ta), gy=h if k % 2 == 0 else o
+        )
     bc[home] = pb[...]
     for k in range(1, nd):
-        d = lax.rem(me + k, nd)
+        d = wrapped(me + k, nd)
         arrived(bc.at[pl.ds(d * own, own)], r_out + d)
 
     sums = jnp.sum(bc[...], axis=0)
     zs[z] = sums
     r_sum = new_recv(gz)
     for k in sorted(range(1, gz), key=lambda k: -min(k, gz - k)):
-        remote(zs.at[z], zs.at[z], r_sum + z, gz=lax.rem(z + k, gz))
+        remote(zs.at[z], zs.at[z], r_sum + z, gz=wrapped(z + k, gz))
     for k in range(half):
         pol[:, 0, k, :] = bc[h * half + k]
     for k in range(1, gz):
-        d = lax.rem(z + k, gz)
+        d = wrapped(z + k, gz)
         arrived(zs.at[d], r_sum + d)
     totals = jnp.sum(zs[...], axis=0)
     sites = float(full * gz * sp.shape[-1])
-    for part in range(2):
-        mean[part] = jnp.sum(totals[part : part + 1, :]) / sites
+    mean[...] = jnp.broadcast_to(jnp.sum(totals, axis=1, keepdims=True) / sites, totals.shape)
 
     for copy in sent:
         copy.wait_send()
@@ -506,17 +525,14 @@
 
         n_send = 2 + 1 + 8 + 1 + 4 + 4 * (STEPS - 1) + 4 + 2 * (nd - 1) + gz - 1
         n_recv = 2 + 4 + 4 + 4 + 2 + 4 + 4 * (STEPS - 1) + 2 * nd + gz
-        return pl.pallas_call(
+        polyakov, means = pl.pallas_call(
             functools.partial(kernel, ta, gz, half),
             out_shape=(
                 jax.ShapeDtypeStruct((2, 1, half, lanes), F32),
-                jax.ShapeDtypeStruct((2,), F32),
+                jax.ShapeDtypeStruct((2, lanes), F32),
             ),
-            in_specs=[pl.BlockSpec(memory_space=pl.ANY)] * 2,
-            out_specs=(
-                pl.BlockSpec(memory_space=pltpu.VMEM),
-                pl.BlockSpec(memory_space=pltpu.SMEM),
-            ),
+            in_specs=[pl.BlockSpec(memory_space=pltpu.HBM)] * 2,
+            out_specs=(pl.BlockSpec(memory_space=pltpu.VMEM),) * 2,
             scratch_shapes=[
                 vmem(STEPS + 1, 4, 2, 3, 3, pad),
                 vmem(2, 3, 3, pad),
@@ -536,12 +552,14 @@
                 pltpu.SemaphoreType.DMA((2,)),
                 pltpu.SemaphoreType.DMA((n_send,)),
                 pltpu.SemaphoreType.DMA((n_recv,)),
-                pltpu.SemaphoreType.REGULAR((max(ta // 2, gz // 2),)),
+                pltpu.SemaphoreType.REGULAR((max(ta // 2, 1),)),
+                pltpu.SemaphoreType.REGULAR((max(gz // 2, 1),)),
             ],
             compiler_params=pltpu.CompilerParams(
-                collective_id=0, has_side_effects=True, vmem_limit_bytes=63 * 1024 * 1024
+                collective_id=0, has_side_effects=True, vmem_limit_bytes=56_450_000
             ),
         )(sp, tl)
+        return polyakov, means[:, 0]
 
     return jax.shard_map(
         body,

time: 88.8 us -> 87.2 us (0.982)
  Pallas kernels: 86.1 us -> 85.2 us
    unnamed x4 -> x1, local copies, waits for them, and re-layouts: 1.81 us -> 0.6 us
    pallas_call x1, Pallas kernels: 86.1 us -> 85.2 us  [body(): pl.pallas_call(functools.partial(kernel, ta, gz, half), out_shape=(jax.Sh...]
where the time goes in v3:
time: 87.2 us; the launch traced here: 87.1 us
  Pallas kernels  85.2 us (98%)
  local copies, waits for them, and re-layouts  1.22 us (1%)
    pallas_call x1, Pallas kernels, body(): pl.pallas_call(functools.partial(kernel, ta, gz, half), out_shape=(jax.Sh...  85.2 us

profile of v3, /device:TPU:65, one launch (start us, length us, event | category | flops | bytes accessed | tf_op | source)
XLA Modules:
  0.0 87.1 jit_solution(15422791438871701375)
XLA Ops:
  0.6 85.2 %shard_map.41 = (f32[2,1,8,128]{3,2,1,0:T(8,128)S(1)}, f32[2,128]{1,0:T(2,128)S(1)}) custom-call(f32[3,2,3,3,2,1,8,128]{7,6,5,4,3,2,1,0:T(8,128)} %sp.1, f32[2,3,3,2,1,8,128]{6,5,4,3,2,1,0:T(8,128)} %tl.1), custom_call_target="tpu_custom_call" | custom-call | tf_op jit(solution)/shard_map/pallas_call | solution.py:528
  85.8 0.6 slice_reduce_fusion
  86.5 0.6 copy.5

commit v4 on v3

--- a/solution.py
+++ b/solution.py
@@ -118,7 +118,7 @@
 def kernel(
     ta, gz, half,
     sp, tl, pol, mean,
-    F, T, H, TH, UP, S, L, AB, M, sm, ar, tree, pb, bc, zs,
+    SP, TL, F, T, H, TH, UP, S, L, AB, M, sm, ar, tree, pb, bc, zs,
     local_sem, send_sem, recv_sem, ready_x, ready_z,
 ):
     def wrapped(v, n):
@@ -159,6 +159,8 @@
         return k
 
     near = [
+        pltpu.make_async_copy(sp, SP, local_sem.at[2]),
+        pltpu.make_async_copy(tl, TL, local_sem.at[3]),
         pltpu.make_async_copy(sp.at[:, :, :, :, h, 0], F.at[0, 0:3, :, :, :, mine], local_sem.at[0]),
         pltpu.make_async_copy(tl.at[:, :, :, h, 0], T.at[:, :, :, mine], local_sem.at[1]),
     ]
@@ -178,6 +180,7 @@
     for dx, dz in around:
         for c in range(2):
             signal(barrier, **place(dx, dz), gy=c)
+    near[0].wait()
     pl.semaphore_wait(barrier, 1 + 2 * len(around))
 
     def relay(sem, rounds, sides):
@@ -207,19 +210,20 @@
     r_own, r_ownt = new_recv(), new_recv()
 
     def plane(f, t):
-        return sp.at[f, :, 0:2, :, t, 0] if f is not None else tl.at[:, 0:2, :, t, 0]
+        return SP.at[f, :, 0:2, :, t, 0] if f is not None else TL.at[:, 0:2, :, t, 0]
 
     def two(ref, *lead):
         return ref.at[(*lead, slice(None), slice(0, 2), slice(None), mine)]
 
     for t in range(2):
         remote(plane(FZ, t), two(F, 0, FV), r_v + h, gz=zp, gy=t)
-    remote(sp.at[:, :, :, :, o, 0], F.at[0, 0:3, :, :, :, mine], r_own, gy=o)
+    remote(SP.at[:, :, :, :, o, 0], F.at[0, 0:3, :, :, :, mine], r_own, gy=o)
     for f, r in ((FX, r_x), (FY, r_y)):
         for t in range(2):
             remote(plane(f, t), two(H, 0, 0, f), r + h, gz=zm, gy=t)
             remote(plane(f, t), two(H, 0, 1, f), r + 2 + h, gz=zp, gy=t)
-    remote(tl.at[:, :, :, o, 0], T.at[:, :, :, mine], r_ownt, gy=o)
+    near[1].wait()
+    remote(TL.at[:, :, :, o, 0], T.at[:, :, :, mine], r_ownt, gy=o)
     for t in range(2):
         remote(plane(None, t), two(TH, 0), r_t + h, gz=zm, gy=t)
     hear_x()
@@ -258,7 +262,7 @@
     def side(ref, s, f, rows, up):
         return ahead_x(load(ref, (s, f), rows)) if up is None else load(ref, (s, f), up)
 
-    def across(s, f):
+    def across(s, f, k):
         def body(rows, up):
             up = None if f == FX else up
             uz, uz_f = load(F, (s, FZ), rows), side(F, s, FZ, rows, up)
@@ -273,7 +277,7 @@
                 total = add(total, load(L, (0,), rows, 2))
             store(F, (s + 1, f), rows, mixed(load(F, (s, f), rows, 2), total, 0.125))
 
-        each_half(body)
+        body(halves[k], pl.ds(k * half + 1, half))
 
     def z_staples(s, f):
         def body(rows, up):
@@ -299,17 +303,18 @@
             unwrap(1)
             unwrap(2)
 
-    def z_links(s):
-        def body(rows, up):
-            for f, k in ((FZ, 1), (FV, 2)):
+    def z_links(s, last):
+        for f, k in ((FZ, 1), (FV, 2)):
+            for part in range(2):
+                rows = halves[part]
                 total = add(load(S, (f,), rows, 2), load(L, (k,), rows, 2))
                 store(F, (s + 1, f), rows, mixed(load(F, (s, f), rows, 2), total, 0.125))
-
-        each_half(body)
+                if last:
+                    onward(s + 1, f, part)
         wrap(F, s + 1, FZ)
         wrap(F, s + 1, FV)
 
-    for copy in near:
+    for copy in near[2:]:
         copy.wait()
     other = pl.ds(pl.multiple_of(o * half, half), half)
     arrived(F.at[0, 0:3, :, :, :, other], r_own)
@@ -325,52 +330,48 @@
     each_half(complete)
     wrap(F, 0, FV)
 
-    r_next = new_recv(4)
-
-    def onward(s, f):
+    r_next = new_recv(8)
+
+    def onward(s, f, k):
         remote(
-            F.at[s, f, :, 0:2, :, 0:full], UP.at[f], r_next + f,
+            F.at[s, f, :, 0:2, :, halves[k]], UP.at[f, :, :, :, halves[k]], r_next + 2 * f + k,
             ta=wrapped(j + h + ta - 1, ta), gy=o,
         )
 
+    def next_arrived(f, k):
+        arrived(UP.at[f, :, :, :, halves[k]], r_next + 2 * f + k)
+
+    r_now = {FX: r_x, FY: r_y}
     for s in range(STEPS):
         last = s == STEPS - 1
-        sems = {}
+        r_then = {f: new_recv(4) for f in (FX, FY)} if not last else {}
         for f in (FX, FY):
-            if s == 0:
+            for k in range(2):
                 for side_k in range(2):
-                    for k in range(2):
-                        arrived(
-                            H.at[0, side_k, f, :, :, :, halves[k]],
-                            (r_x, r_y)[f] + 2 * side_k + k,
+                    arrived(H.at[s, side_k, f, :, :, :, halves[k]], r_now[f] + 2 * side_k + k)
+                across(s, f, k)
+                if last:
+                    onward(s + 1, f, k)
+                else:
+                    out = F.at[s + 1, f, :, 0:2, :, halves[k]]
+                    for side_k, to in ((0, zm), (1, zp)):
+                        remote(
+                            out, H.at[s + 1, side_k, f, :, :, :, halves[k]],
+                            r_then[f] + 2 * side_k + k, gz=to,
                         )
-            else:
-                for side_k in range(2):
-                    arrived(H.at[s, side_k, f], r_now[f] + side_k)
-            across(s, f)
             if f == FX:
                 wrap(F, s + 1, FX)
-            if last:
-                onward(s + 1, f)
             else:
-                sems[f] = new_recv(2)
-                out = F.at[s + 1, f, :, 0:2, :, 0:full]
-                remote(out, H.at[s + 1, 0, f], sems[f], gz=zm)
-                remote(out, H.at[s + 1, 1, f], sems[f] + 1, gz=zp)
-            if f == FY:
                 hear_x(last)
             if last:
                 hear_z()
             z_staples(s, f)
-        r_now = sems
+        r_now = r_then
         if s == STEPS - 2:
             for t in range(2):
                 remote(plane(None, t), two(TH, 1), r_t + 2 + h, gz=zp, gy=t)
-        z_links(s)
-        if last:
-            onward(s + 1, FZ)
-            onward(s + 1, FV)
-        else:
+        z_links(s, last)
+        if not last:
             in_plane(s + 1)
 
     n = STEPS
@@ -394,8 +395,10 @@
 
     each_half(before)
     hear_z()
-    arrived(UP.at[FX], r_next + FX)
-    arrived(UP.at[FY], r_next + FY)
+    for k in range(2):
+        next_arrived(FX, k)
+    for k in range(2):
+        next_arrived(FY, k)
 
     def along_xy(rows, up):
         ux, uy = load2(UP, (FX,), rows), load2(UP, (FY,), rows)
@@ -410,8 +413,10 @@
     each_half(along_xy)
     hear_z()
     unwrap(0)
-    arrived(UP.at[FZ], r_next + FZ)
-    arrived(UP.at[FV], r_next + FV)
+    for k in range(2):
+        next_arrived(FZ, k)
+    for k in range(2):
+        next_arrived(FV, k)
 
     def finish(k, carry):
         r0 = pl.multiple_of(k * half, half)
@@ -523,8 +528,8 @@
         def vmem(*dims):
             return pltpu.VMEM((*dims, lanes), F32)
 
-        n_send = 2 + 1 + 8 + 1 + 4 + 4 * (STEPS - 1) + 4 + 2 * (nd - 1) + gz - 1
-        n_recv = 2 + 4 + 4 + 4 + 2 + 4 + 4 * (STEPS - 1) + 2 * nd + gz
+        n_send = 2 + 1 + 8 + 1 + 4 + 8 * (STEPS - 1) + 8 + 2 * (nd - 1) + gz - 1
+        n_recv = 2 + 4 + 4 + 4 + 2 + 8 + 8 * (STEPS - 1) + 2 * nd + gz
         polyakov, means = pl.pallas_call(
             functools.partial(kernel, ta, gz, half),
             out_shape=(
@@ -534,6 +539,8 @@
             in_specs=[pl.BlockSpec(memory_space=pltpu.HBM)] * 2,
             out_specs=(pl.BlockSpec(memory_space=pltpu.VMEM),) * 2,
             scratch_shapes=[
+                pltpu.VMEM(sp.shape, F32),
+                pltpu.VMEM(tl.shape, F32),
                 vmem(STEPS + 1, 4, 2, 3, 3, pad),
                 vmem(2, 3, 3, pad),
                 vmem(STEPS, 2, 2, 2, 2, 3, full),
@@ -549,7 +556,7 @@
                 vmem(own, 2),
                 vmem(full, 2),
                 vmem(gz, 2),
-                pltpu.SemaphoreType.DMA((2,)),
+                pltpu.SemaphoreType.DMA((4,)),
                 pltpu.SemaphoreType.DMA((n_send,)),
                 pltpu.SemaphoreType.DMA((n_recv,)),
                 pltpu.SemaphoreType.REGULAR((max(ta // 2, 1),)),

time: 87.2 us -> 85.6 us (0.982)
  Pallas kernels: 85.2 us -> 83.6 us
    pallas_call x1, Pallas kernels: 85.2 us -> 83.6 us  [body(): pl.pallas_call(functools.partial(kernel, ta, gz, half), out_shape=(jax.Sh...]
where the time goes in v4:
time: 85.6 us; the launch traced here: 85.5 us
  Pallas kernels  83.6 us (98%)
  local copies, waits for them, and re-layouts  1.22 us (1%)
    pallas_call x1, Pallas kernels, body(): pl.pallas_call(functools.partial(kernel, ta, gz, half), out_shape=(jax.Sh...  83.6 us

profile of v4, /device:TPU:65, one launch (start us, length us, event | category | flops | bytes accessed | tf_op | source)
XLA Modules:
  0.0 85.5 jit_solution(12160597399257972280)
XLA Ops:
  0.6 83.6 %shard_map.41 = (f32[2,1,8,128]{3,2,1,0:T(8,128)S(1)}, f32[2,128]{1,0:T(2,128)S(1)}) custom-call(f32[3,2,3,3,2,1,8,128]{7,6,5,4,3,2,1,0:T(8,128)} %sp.1, f32[2,3,3,2,1,8,128]{6,5,4,3,2,1,0:T(8,128)} %tl.1), custom_call_target="tpu_custom_call" | custom-call | tf_op jit(solution)/shard_map/pallas_call | solution.py:533
  84.3 0.6 slice_reduce_fusion
  84.9 0.6 copy.5

commit v5 on v4

--- a/solution.py
+++ b/solution.py
@@ -1,4 +1,5 @@
 import functools
+import math
 
 import jax
 import jax.numpy as jnp
@@ -134,28 +135,25 @@
     mine = pl.ds(pl.multiple_of(h * half, half), half)
     halves = [pl.ds(k * half, half) for k in range(2)]
 
-    sent = []
-    n_sem = [0, 0]
+    rows_sent = [0]
+    n_recv = [0]
 
     def remote(src, dst, recv_index, **where):
-        k = n_sem[0]
-        n_sem[0] += 1
-        copy = pltpu.make_async_remote_copy(
-            src_ref=src, dst_ref=dst, send_sem=send_sem.at[k], recv_sem=recv_sem.at[recv_index],
+        pltpu.make_async_remote_copy(
+            src_ref=src, dst_ref=dst, send_sem=send_sem, recv_sem=recv_sem.at[recv_index],
             device_id=where, device_id_type=MESH,
-        )
-        copy.start()
-        sent.append(copy)
+        ).start()
+        rows_sent[0] += math.prod(src.shape[:-1])
 
     def arrived(dst, recv_index):
         pltpu.make_async_remote_copy(
-            src_ref=dst, dst_ref=dst, send_sem=send_sem.at[0], recv_sem=recv_sem.at[recv_index],
+            src_ref=dst, dst_ref=dst, send_sem=send_sem, recv_sem=recv_sem.at[recv_index],
             device_id={"gy": o}, device_id_type=MESH,
         ).wait_recv()
 
     def new_recv(n=1):
-        k = n_sem[1]
-        n_sem[1] += n
+        k = n_recv[0]
+        n_recv[0] += n
         return k
 
     near = [
@@ -168,7 +166,7 @@
         copy.start()
 
     barrier = pltpu.get_barrier_semaphore()
-    around = sorted({(0, 1 % gz), (0, (gz - 1) % gz), (1 % ta, 0), ((ta - 1) % ta, 0)} - {(0, 0)})
+    around = sorted({(0, 1 % gz), (0, gz - 1), (1 % ta, 0), (ta - 1, 0)} - {(0, 0)})
 
     def place(dx, dz):
         return {"ta": wrapped(j + dx, ta), "gz": wrapped(z + dz, gz)}
@@ -206,7 +204,7 @@
         ready_z, gz // 2 - STEPS, [{"gz": wrapped(z + k, gz)} for k in sorted({1 % gz, gz - 1} - {0})]
     )
 
-    r_v, r_x, r_y, r_t = new_recv(2), new_recv(4), new_recv(4), new_recv(4)
+    r_v, r_x, r_y, r_t = new_recv(2), new_recv(2), new_recv(2), new_recv(2)
     r_own, r_ownt = new_recv(), new_recv()
 
     def plane(f, t):
@@ -221,7 +219,7 @@
     for f, r in ((FX, r_x), (FY, r_y)):
         for t in range(2):
             remote(plane(f, t), two(H, 0, 0, f), r + h, gz=zm, gy=t)
-            remote(plane(f, t), two(H, 0, 1, f), r + 2 + h, gz=zp, gy=t)
+            remote(plane(f, t), two(H, 0, 1, f), r + h, gz=zp, gy=t)
     near[1].wait()
     remote(TL.at[:, :, :, o, 0], T.at[:, :, :, mine], r_ownt, gy=o)
     for t in range(2):
@@ -330,25 +328,21 @@
     each_half(complete)
     wrap(F, 0, FV)
 
-    r_next = new_recv(8)
+    r_next = new_recv(4)
 
     def onward(s, f, k):
         remote(
-            F.at[s, f, :, 0:2, :, halves[k]], UP.at[f, :, :, :, halves[k]], r_next + 2 * f + k,
+            F.at[s, f, :, 0:2, :, halves[k]], UP.at[f, :, :, :, halves[k]], r_next + f,
             ta=wrapped(j + h + ta - 1, ta), gy=o,
         )
-
-    def next_arrived(f, k):
-        arrived(UP.at[f, :, :, :, halves[k]], r_next + 2 * f + k)
 
     r_now = {FX: r_x, FY: r_y}
     for s in range(STEPS):
         last = s == STEPS - 1
-        r_then = {f: new_recv(4) for f in (FX, FY)} if not last else {}
+        r_then = {f: new_recv(2) for f in (FX, FY)} if not last else {}
         for f in (FX, FY):
             for k in range(2):
-                for side_k in range(2):
-                    arrived(H.at[s, side_k, f, :, :, :, halves[k]], r_now[f] + 2 * side_k + k)
+                arrived(H.at[s, :, f, :, :, :, halves[k]], r_now[f] + k)
                 across(s, f, k)
                 if last:
                     onward(s + 1, f, k)
@@ -357,7 +351,7 @@
                     for side_k, to in ((0, zm), (1, zp)):
                         remote(
                             out, H.at[s + 1, side_k, f, :, :, :, halves[k]],
-                            r_then[f] + 2 * side_k + k, gz=to,
+                            r_then[f] + k, gz=to,
                         )
             if f == FX:
                 wrap(F, s + 1, FX)
@@ -369,7 +363,7 @@
         r_now = r_then
         if s == STEPS - 2:
             for t in range(2):
-                remote(plane(None, t), two(TH, 1), r_t + 2 + h, gz=zp, gy=t)
+                remote(plane(None, t), two(TH, 1), r_t + h, gz=zp, gy=t)
         z_links(s, last)
         if not last:
             in_plane(s + 1)
@@ -377,9 +371,8 @@
     n = STEPS
     arrived(T.at[:, :, :, other], r_ownt)
     wrap(T)
-    for side_k in range(2):
-        for k in range(2):
-            arrived(TH.at[side_k, :, :, :, halves[k]], r_t + 2 * side_k + k)
+    for k in range(2):
+        arrived(TH.at[:, :, :, :, halves[k]], r_t + k)
 
     def before(rows, up):
         t = load(T, (), rows)
@@ -395,10 +388,8 @@
 
     each_half(before)
     hear_z()
-    for k in range(2):
-        next_arrived(FX, k)
-    for k in range(2):
-        next_arrived(FY, k)
+    arrived(UP.at[FX], r_next + FX)
+    arrived(UP.at[FY], r_next + FY)
 
     def along_xy(rows, up):
         ux, uy = load2(UP, (FX,), rows), load2(UP, (FY,), rows)
@@ -413,10 +404,8 @@
     each_half(along_xy)
     hear_z()
     unwrap(0)
-    for k in range(2):
-        next_arrived(FZ, k)
-    for k in range(2):
-        next_arrived(FV, k)
+    arrived(UP.at[FZ], r_next + FZ)
+    arrived(UP.at[FV], r_next + FV)
 
     def finish(k, carry):
         r0 = pl.multiple_of(k * half, half)
@@ -439,7 +428,7 @@
 
     span = own * 16
     sm3, ar3 = sm.reshape(full, 16, sm.shape[-1]), ar.reshape(full, 16, sm.shape[-1])
-    r_row = new_recv(nd)
+    r_row = new_recv()
     offsets = sorted(range(1, nd), key=lambda k: -min(k // 2, ta - k // 2))
     here = pl.ds(me * own, own)
 
@@ -448,12 +437,10 @@
 
     for k in offsets:
         dj, dh = wrapped(j + k // 2, ta), (h if k % 2 == 0 else o)
-        remote(part_of(sm3, 2 * dj + dh), part_of(ar3, me), r_row + me, ta=dj, gy=dh)
+        remote(part_of(sm3, 2 * dj + dh), part_of(ar3, me), r_row, ta=dj, gy=dh)
     hear_z()
     ar3[here] = sm3[here]
-    for k in range(1, nd):
-        d = wrapped(me + k, nd)
-        arrived(part_of(ar3, d), r_row + d)
+    arrived(ar3.at[pl.ds(0, full - own), 0:12], r_row)
 
     def slices(start, stride, rows):
         at = lambda c: ar[pl.ds(start + c, rows, stride), :]
@@ -486,33 +473,29 @@
         pb[row, 1:2, :] = im / 3.0
 
     hear_z(True)
-    r_out = new_recv(nd)
+    r_out = new_recv()
     home = pl.ds(me * own, own)
     for k in offsets:
         remote(
-            pb, bc.at[home], r_out + me, ta=wrapped(j + k // 2, ta), gy=h if k % 2 == 0 else o
+            pb, bc.at[home], r_out, ta=wrapped(j + k // 2, ta), gy=h if k % 2 == 0 else o
         )
     bc[home] = pb[...]
-    for k in range(1, nd):
-        d = wrapped(me + k, nd)
-        arrived(bc.at[pl.ds(d * own, own)], r_out + d)
+    arrived(bc.at[pl.ds(0, full - own)], r_out)
 
     sums = jnp.sum(bc[...], axis=0)
     zs[z] = sums
-    r_sum = new_recv(gz)
+    r_sum = new_recv()
     for k in sorted(range(1, gz), key=lambda k: -min(k, gz - k)):
-        remote(zs.at[z], zs.at[z], r_sum + z, gz=wrapped(z + k, gz))
+        remote(zs.at[z], zs.at[z], r_sum, gz=wrapped(z + k, gz))
     for k in range(half):
         pol[:, 0, k, :] = bc[h * half + k]
-    for k in range(1, gz):
-        d = wrapped(z + k, gz)
-        arrived(zs.at[d], r_sum + d)
+    arrived(zs.at[pl.ds(0, gz - 1)], r_sum)
     totals = jnp.sum(zs[...], axis=0)
     sites = float(full * gz * sp.shape[-1])
     mean[...] = jnp.broadcast_to(jnp.sum(totals, axis=1, keepdims=True) / sites, totals.shape)
 
-    for copy in sent:
-        copy.wait_send()
+    lines = F.reshape(math.prod(F.shape[:-1]), F.shape[-1]).at[pl.ds(0, rows_sent[0])]
+    pltpu.make_async_copy(lines, lines, send_sem).wait()
 
 
 def solution(mesh):
@@ -528,8 +511,7 @@
         def vmem(*dims):
             return pltpu.VMEM((*dims, lanes), F32)
 
-        n_send = 2 + 1 + 8 + 1 + 4 + 8 * (STEPS - 1) + 8 + 2 * (nd - 1) + gz - 1
-        n_recv = 2 + 4 + 4 + 4 + 2 + 8 + 8 * (STEPS - 1) + 2 * nd + gz
+        n_recv = 2 + 2 + 2 + 2 + 2 + 4 + 4 * (STEPS - 1) + 3
         polyakov, means = pl.pallas_call(
             functools.partial(kernel, ta, gz, half),
             out_shape=(
@@ -557,7 +539,7 @@
                 vmem(full, 2),
                 vmem(gz, 2),
                 pltpu.SemaphoreType.DMA((4,)),
-                pltpu.SemaphoreType.DMA((n_send,)),
+                pltpu.SemaphoreType.DMA,
                 pltpu.SemaphoreType.DMA((n_recv,)),
                 pltpu.SemaphoreType.REGULAR((max(ta // 2, 1),)),
                 pltpu.SemaphoreType.REGULAR((max(gz // 2, 1),)),

time: 85.6 us -> 84.1 us (0.982)
  Pallas kernels: 83.6 us -> 82.1 us
    pallas_call x1, Pallas kernels: 83.6 us -> 82.1 us  [body(): pl.pallas_call(functools.partial(kernel, ta, gz, half), out_shape=(jax.Sh...]
where the time goes in v5:
time: 84.1 us; the launch traced here: 84 us
  Pallas kernels  82.1 us (98%)
  local copies, waits for them, and re-layouts  1.22 us (1%)
    pallas_call x1, Pallas kernels, body(): pl.pallas_call(functools.partial(kernel, ta, gz, half), out_shape=(jax.Sh...  82.1 us

profile of v5, /device:TPU:65, one launch (start us, length us, event | category | flops | bytes accessed | tf_op | source)
XLA Modules:
  0.0 84.0 jit_solution(5776890827584665821)
XLA Ops:
  0.6 82.1 %shard_map.41 = (f32[2,1,8,128]{3,2,1,0:T(8,128)S(1)}, f32[2,128]{1,0:T(2,128)S(1)}) custom-call(f32[3,2,3,3,2,1,8,128]{7,6,5,4,3,2,1,0:T(8,128)} %sp.1, f32[2,3,3,2,1,8,128]{6,5,4,3,2,1,0:T(8,128)} %tl.1), custom_call_target="tpu_custom_call" | custom-call | tf_op jit(solution)/shard_map/pallas_call | solution.py:515
  82.8 0.6 slice_reduce_fusion
  83.4 0.6 copy.5

commit v6 on v5

--- a/solution.py
+++ b/solution.py
@@ -130,20 +130,21 @@
     zp, zm = wrapped(z + 1, gz), wrapped(z + gz - 1, gz)
     full = 2 * half
     nd = 2 * ta
-    own = full // nd
+    own = full // ta
     me = 2 * j + h
     mine = pl.ds(pl.multiple_of(h * half, half), half)
     halves = [pl.ds(k * half, half) for k in range(2)]
 
-    rows_sent = [0]
+    rows_sent = [0, 0]
     n_recv = [0]
 
-    def remote(src, dst, recv_index, **where):
+    def remote(src, dst, recv_index, cores=(0, 1), **where):
         pltpu.make_async_remote_copy(
             src_ref=src, dst_ref=dst, send_sem=send_sem, recv_sem=recv_sem.at[recv_index],
             device_id=where, device_id_type=MESH,
         ).start()
-        rows_sent[0] += math.prod(src.shape[:-1])
+        for c in cores:
+            rows_sent[c] += math.prod(src.shape[:-1])
 
     def arrived(dst, recv_index):
         pltpu.make_async_remote_copy(
@@ -426,42 +427,53 @@
 
     lax.fori_loop(0, 2, finish, 0)
 
-    span = own * 16
-    sm3, ar3 = sm.reshape(full, 16, sm.shape[-1]), ar.reshape(full, 16, sm.shape[-1])
-    r_row = new_recv()
-    offsets = sorted(range(1, nd), key=lambda k: -min(k // 2, ta - k // 2))
-    here = pl.ds(me * own, own)
-
-    def part_of(ref, d):
-        return ref.at[pl.ds(d * own, own), 0:12]
-
-    for k in offsets:
-        dj, dh = wrapped(j + k // 2, ta), (h if k % 2 == 0 else o)
-        remote(part_of(sm3, 2 * dj + dh), part_of(ar3, me), r_row, ta=dj, gy=dh)
+    lanes = sm.shape[-1]
+    sm3, ar3 = sm.reshape(full, 16, lanes), ar.reshape(own * nd, 16, lanes)
+    ar4 = ar.reshape(own, nd, 16, lanes)
+    r_row, r_out = new_recv(), new_recv()
+    away = sorted(range(1, ta), key=lambda k: -min(k, ta - k))
+    home = pl.ds(j * own, own)
+
+    def to_product(k, **kw):
+        jd = wrapped(j + k, ta) if k else j
+        remote(
+            sm3.at[pl.ds(jd * own, own), 0:12], ar4.at[:, me, 0:12], r_row, ta=jd, gy=1, **kw
+        )
+
+    for k in away:
+        to_product(k)
+
+    @pl.when(h == 0)
+    def _():
+        to_product(0, cores=(0,))
+
     hear_z()
-    ar3[here] = sm3[here]
-    arrived(ar3.at[pl.ds(0, full - own), 0:12], r_row)
-
-    def slices(start, stride, rows):
-        at = lambda c: ar[pl.ds(start + c, rows, stride), :]
+
+    def slices(start, rows):
+        at = lambda c: ar[pl.ds(start + c, rows, 32), :]
         return third_row(
             tuple([[at(part * 6 + a * 3 + b) for b in range(3)] for a in range(2)] for part in range(2))
         )
 
-    for row in range(own):
-        rows = nd // 2
-        lhs, rhs = slices(row * 16, 2 * span, rows), slices(row * 16 + span, 2 * span, rows)
-        while rows > 1:
-            prod = mul(lhs, rhs)
-            flat = [v for part in prod for line in part for v in line]
+    def pick(first, rows):
+        vs = [tree[pl.ds(c * full + first, rows, 2), :] for c in range(18)]
+        return tuple(
+            [[vs[part * 9 + a * 3 + b] for b in range(3)] for a in range(3)] for part in range(2)
+        )
+
+    @pl.when(h == 1)
+    def _():
+        for r in range(own):
+            ar3[r * nd + me] = sm3[j * own + r]
+        arrived(ar4.at[:, 0 : nd - 1, 0:12], r_row)
+        rows = own * nd // 2
+        lhs, rhs = slices(0, rows), slices(16, rows)
+        while rows > own:
+            flat = [v for part in mul(lhs, rhs) for line in part for v in line]
             for c, v in enumerate(flat):
-                tree[pl.ds(c * 8, rows), :] = v
+                tree[pl.ds(c * full, rows), :] = v
             rows //= 2
-            pick = lambda first: [tree[pl.ds(c * 8 + first, rows, 2), :] for c in range(18)]
-            grid = lambda vs: tuple(
-                [[vs[part * 9 + a * 3 + b] for b in range(3)] for a in range(3)] for part in range(2)
-            )
-            lhs, rhs = grid(pick(0)), grid(pick(1))
+            lhs, rhs = pick(0, rows), pick(1, rows)
         re = im = None
         for a in range(3):
             for b in range(3):
@@ -469,19 +481,21 @@
                 t_re, t_im = lr * rr - li * ri, lr * ri + li * rr
                 re = t_re if re is None else re + t_re
                 im = t_im if im is None else im + t_im
-        pb[row, 0:1, :] = re / 3.0
-        pb[row, 1:2, :] = im / 3.0
+        for r in range(own):
+            pb[r, 0:1, :] = re[r : r + 1] / 3.0
+            pb[r, 1:2, :] = im[r : r + 1] / 3.0
+        for k in away:
+            for c in range(2):
+                remote(pb, bc.at[home], r_out, cores=(1,), ta=wrapped(j + k, ta), gy=c)
+        remote(pb, bc.at[home], r_out, cores=(1,), gy=0)
+        bc[home] = pb[...]
+        arrived(bc.at[pl.ds(0, full - own)], r_out)
+
+    @pl.when(h == 0)
+    def _():
+        arrived(bc, r_out)
 
     hear_z(True)
-    r_out = new_recv()
-    home = pl.ds(me * own, own)
-    for k in offsets:
-        remote(
-            pb, bc.at[home], r_out, ta=wrapped(j + k // 2, ta), gy=h if k % 2 == 0 else o
-        )
-    bc[home] = pb[...]
-    arrived(bc.at[pl.ds(0, full - own)], r_out)
-
     sums = jnp.sum(bc[...], axis=0)
     zs[z] = sums
     r_sum = new_recv()
@@ -494,8 +508,12 @@
     sites = float(full * gz * sp.shape[-1])
     mean[...] = jnp.broadcast_to(jnp.sum(totals, axis=1, keepdims=True) / sites, totals.shape)
 
-    lines = F.reshape(math.prod(F.shape[:-1]), F.shape[-1]).at[pl.ds(0, rows_sent[0])]
-    pltpu.make_async_copy(lines, lines, send_sem).wait()
+    def all_sent(c):
+        lines = F.reshape(math.prod(F.shape[:-1]), lanes).at[pl.ds(0, rows_sent[c])]
+        pltpu.make_async_copy(lines, lines, send_sem).wait()
+
+    for c in range(2):
+        pl.when(h == c)(functools.partial(all_sent, c))
 
 
 def solution(mesh):
@@ -505,8 +523,7 @@
         half, lanes = sp.shape[-2:]
         full = 2 * half
         pad = full + 8
-        nd = 2 * ta
-        own = full // nd
+        own = full // ta
 
         def vmem(*dims):
             return pltpu.VMEM((*dims, lanes), F32)
@@ -533,8 +550,8 @@
                 vmem(2, 2, 3, 3, full),
                 vmem(6, 2, 2, 3, full),
                 vmem(full * 16),
-                vmem(full * 16),
-                vmem(18 * 8),
+                vmem(2 * full * 16),
+                vmem(18 * full),
                 vmem(own, 2),
                 vmem(full, 2),
                 vmem(gz, 2),

time: 84.1 us -> 83.4 us (level)
  no operation moved by 1% of the time
where the time goes in v6:
time: 83.4 us; the launch traced here: 83.2 us
  Pallas kernels  81.4 us (98%)
  local copies, waits for them, and re-layouts  1.22 us (1%)
    pallas_call x1, Pallas kernels, body(): pl.pallas_call(functools.partial(kernel, ta, gz, half), out_shape=(jax.Sh...  81.4 us

profile of v6, /device:TPU:65, one launch (start us, length us, event | category | flops | bytes accessed | tf_op | source)
XLA Modules:
  0.0 83.2 jit_solution(12582606316718452017)
XLA Ops:
  0.6 81.4 %shard_map.41 = (f32[2,1,8,128]{3,2,1,0:T(8,128)S(1)}, f32[2,128]{1,0:T(2,128)S(1)}) custom-call(f32[3,2,3,3,2,1,8,128]{7,6,5,4,3,2,1,0:T(8,128)} %sp.1, f32[2,3,3,2,1,8,128]{6,5,4,3,2,1,0:T(8,128)} %tl.1), custom_call_target="tpu_custom_call" | custom-call | tf_op jit(solution)/shard_map/pallas_call | solution.py:532
  82.0 0.6 slice_reduce_fusion
  82.6 0.6 copy.5

commit v7 on v6

--- a/solution.py
+++ b/solution.py
@@ -119,7 +119,7 @@
 def kernel(
     ta, gz, half,
     sp, tl, pol, mean,
-    SP, TL, F, T, H, TH, UP, S, L, AB, M, sm, ar, tree, pb, bc, zs,
+    SP, TL, F, T, H, TH, UP, TB, THB, YP, YQ, Q, S, L, AB, M, sm, ar, tree, pb, bc, zs,
     local_sem, send_sem, recv_sem, ready_x, ready_z,
 ):
     def wrapped(v, n):
@@ -329,13 +329,24 @@
     each_half(complete)
     wrap(F, 0, FV)
 
-    r_next = new_recv(4)
+    r_next = [new_recv(5), new_recv(5)]
+    r_tb, r_thb = new_recv(), new_recv()
+    beside = [{"ta": wrapped(j + h + ta - 1, ta), "gy": o}, {"ta": wrapped(j + h, ta), "gy": o}]
+    inner = pl.ds(half, half)
 
     def onward(s, f, k):
         remote(
-            F.at[s, f, :, 0:2, :, halves[k]], UP.at[f, :, :, :, halves[k]], r_next + f,
-            ta=wrapped(j + h + ta - 1, ta), gy=o,
+            F.at[s, f, :, 0:2, :, halves[k]], UP.at[k, f, :, :, :, inner], r_next[k] + f, **beside[k]
         )
+
+    def entries():
+        return [(part, a, b) for part in range(2) for a in range(2) for b in range(3)]
+
+    def onward_row(s, k):
+        row = full - 1 if k == 0 else half - 1
+        for c, (part, a, b) in enumerate(entries()):
+            YP[k, pl.ds(c, 1), :] = F[s, FY, part, a, b, pl.ds(row, 1), :]
+        remote(YP.at[k, 0:12], YQ.at[k, 0:12], r_next[k] + 4, **beside[k])
 
     r_now = {FX: r_x, FY: r_y}
     for s in range(STEPS):
@@ -357,75 +368,119 @@
             if f == FX:
                 wrap(F, s + 1, FX)
             else:
+                if last:
+                    for k in range(2):
+                        onward_row(s + 1, k)
                 hear_x(last)
             if last:
                 hear_z()
             z_staples(s, f)
         r_now = r_then
+        if s == 0:
+            arrived(T.at[:, :, :, other], r_ownt)
+            wrap(T)
+            remote(T.at[:, 0:2, :, 0:full], TB.at[:, :, :, 0:full], r_tb, **beside[1])
         if s == STEPS - 2:
             for t in range(2):
                 remote(plane(None, t), two(TH, 1), r_t + h, gz=zp, gy=t)
+
+            @pl.when(h == 1)
+            def _():
+                for side_k, to in ((0, zm), (1, zp)):
+                    for t in range(2):
+                        remote(
+                            plane(None, t), THB.at[side_k], r_thb, cores=(1,),
+                            ta=wrapped(j + t, ta), gz=to, gy=1 - t,
+                        )
         z_links(s, last)
         if not last:
             in_plane(s + 1)
 
     n = STEPS
-    arrived(T.at[:, :, :, other], r_ownt)
-    wrap(T)
+    r0, r1 = halves
+    before1 = pl.ds(half - 1, half)
     for k in range(2):
         arrived(TH.at[:, :, :, :, halves[k]], r_t + k)
 
-    def before(rows, up):
-        t = load(T, (), rows)
-        ux, uy = load(F, (n, FX), rows), load(F, (n, FY), rows)
-        store(M, (0,), rows, mul(ux, ahead_x(t), rows=2))
-        store(M, (1,), rows, mul(ux, t, da=True, rows=2))
-        store(M, (2,), rows, mul(uy, load(T, (), up), rows=2))
-        store(M, (3,), rows, mul(uy, t, da=True, rows=2))
-        store(M, (4,), rows, mul(load(F, (n, FZ), rows), load2(TH, (0,), rows), rows=2))
-        store(
-            M, (5,), rows, mul(load(F, (n, FV), rows), load2(TH, (1,), rows), da=True, rows=2)
-        )
-
-    each_half(before)
+    def lower_y(rows, up):
+        store(M, (3,), up, mul(load(F, (n, FY), rows), load(T, (), rows), da=True, rows=2))
+
+    each_half(lower_y)
+    M[3, :, :, :, pl.ds(0, 1)] = M[3, :, :, :, pl.ds(full, 1)]
+    t = load(T, (), r0)
+    ux, uy = load(F, (n, FX), r0), load(F, (n, FY), r0)
+    store(M, (0,), r0, mul(ux, ahead_x(t), rows=2))
+    store(M, (1,), r0, mul(ux, t, da=True, rows=2))
+    store(M, (2,), r0, mul(uy, load(T, (), pl.ds(1, half)), rows=2))
+    store(M, (4,), r0, mul(load(F, (n, FZ), r0), load2(TH, (0,), r0), rows=2))
+    store(M, (5,), r0, mul(load(F, (n, FV), r0), load2(TH, (1,), r0), da=True, rows=2))
+
+    arrived(TB.at[:, :, :, 0:full], r_tb)
+    wrap(TB)
+    arrived(THB, r_thb)
+    t = load2(TB, (), r1)
+    ux = load(F, (n, FX), r1)
+    store(Q, (0,), r0, mul(ahead_x(t), ux, db=True))
+    store(Q, (1,), r0, mul(t, ux))
+    store(Q, (2,), r0, mul(load2(TB, (), pl.ds(half + 1, half)), load(F, (n, FY), r1), db=True))
+    store(Q, (3,), r0, mul(load2(TB, (), before1), load(F, (n, FY), before1)))
+    store(Q, (4,), r0, mul(load2(THB, (0,), r0), load(F, (n, FZ), r1), db=True))
+    store(Q, (5,), r0, mul(load2(THB, (1,), r0), load(F, (n, FV), r1)))
     hear_z()
-    arrived(UP.at[FX], r_next + FX)
-    arrived(UP.at[FY], r_next + FY)
-
-    def along_xy(rows, up):
-        ux, uy = load2(UP, (FX,), rows), load2(UP, (FY,), rows)
-        total = add(
-            mul(load(M, (0,), rows, 2), ux, db=True, rows=2),
-            back_x(mul(load(M, (1,), rows, 2), ux, rows=2)),
-            mul(load(M, (2,), rows, 2), uy, db=True, rows=2),
-        )
-        store(S, (0,), rows, total)
-        store(L, (0,), up, mul(load(M, (3,), rows, 2), uy, rows=2))
-
-    each_half(along_xy)
-    hear_z()
-    unwrap(0)
-    arrived(UP.at[FZ], r_next + FZ)
-    arrived(UP.at[FV], r_next + FV)
-
-    def finish(k, carry):
-        r0 = pl.multiple_of(k * half, half)
-        rows = pl.ds(r0, half)
-        uz, uv = load2(UP, (FZ,), rows), load2(UP, (FV,), rows)
-        total = add(
-            load(S, (0,), rows, 2),
-            load(L, (0,), rows, 2),
-            mul(load(M, (4,), rows, 2), uz, db=True, rows=2),
-            mul(load(M, (5,), rows, 2), uv, rows=2),
-        )
-        done = mixed(load(T, (), rows, 2), total, 0.5 / 6.0)
-        for part in range(2):
-            for a in range(2):
-                for b in range(3):
-                    sm[pl.ds(r0 * 16 + part * 6 + a * 3 + b, half, 16), :] = done[part][a][b]
-        return carry
-
-    lax.fori_loop(0, 2, finish, 0)
+
+    def came(k, f):
+        arrived(UP.at[k, f, :, :, :, inner], r_next[k] + f)
+
+    def row_came(k):
+        arrived(YQ.at[k, 0:12], r_next[k] + 4)
+        for c, (part, a, b) in enumerate(entries()):
+            UP[k, FY, part, a, b, pl.ds(half - 1, 1), :] = YQ[k, pl.ds(c, 1), :]
+
+    for k in range(2):
+        came(k, FX)
+        came(k, FY)
+        row_came(k)
+        if k == 0:
+            ux = load2(UP, (0, FX), inner)
+            total = add(
+                mul(load(M, (0,), r0, 2), ux, db=True, rows=2),
+                back_x(mul(load(M, (1,), r0, 2), ux, rows=2)),
+                mul(load(M, (2,), r0, 2), load2(UP, (0, FY), inner), db=True, rows=2),
+                mul(load(M, (3,), r0, 2), load2(UP, (0, FY), before1), rows=2),
+            )
+        else:
+            ux = load2(UP, (1, FX), inner)
+            total = add(
+                mul(ux, load(Q, (0,), r0), rows=2),
+                back_x(mul(ux, load(Q, (1,), r0), da=True, rows=2)),
+                mul(load2(UP, (1, FY), inner), load(Q, (2,), r0), rows=2),
+                mul(load2(UP, (1, FY), before1), load(Q, (3,), r0), da=True, rows=2),
+            )
+        store(S, (0,), halves[k], total)
+        if k == 0:
+            hear_z()
+
+    for k in range(2):
+        came(k, FZ)
+        came(k, FV)
+        uz, uv = load2(UP, (k, FZ), inner), load2(UP, (k, FV), inner)
+        if k == 0:
+            link = load(T, (), r0, 2)
+            total = add(
+                load(S, (0,), r0, 2),
+                mul(load(M, (4,), r0, 2), uz, db=True, rows=2),
+                mul(load(M, (5,), r0, 2), uv, rows=2),
+            )
+        else:
+            link = load(TB, (), r1, 2)
+            total = add(
+                load(S, (0,), r1, 2),
+                mul(uz, load(Q, (4,), r0), rows=2),
+                mul(uv, load(Q, (5,), r0), da=True, rows=2),
+            )
+        done = mixed(link, total, 0.5 / 6.0)
+        for c, (part, a, b) in enumerate(entries()):
+            sm[pl.ds(k * half * 16 + c, half, 16), :] = done[part][a][b]
 
     lanes = sm.shape[-1]
     sm3, ar3 = sm.reshape(full, 16, lanes), ar.reshape(own * nd, 16, lanes)
@@ -434,10 +489,14 @@
     away = sorted(range(1, ta), key=lambda k: -min(k, ta - k))
     home = pl.ds(j * own, own)
 
+    def slice_of(jd):
+        return jnp.where(jd * own < half, me, wrapped(me + nd - 1, nd))
+
     def to_product(k, **kw):
         jd = wrapped(j + k, ta) if k else j
         remote(
-            sm3.at[pl.ds(jd * own, own), 0:12], ar4.at[:, me, 0:12], r_row, ta=jd, gy=1, **kw
+            sm3.at[pl.ds(jd * own, own), 0:12], ar4.at[:, slice_of(jd), 0:12], r_row,
+            ta=jd, gy=1, **kw,
         )
 
     for k in away:
@@ -464,7 +523,7 @@
     @pl.when(h == 1)
     def _():
         for r in range(own):
-            ar3[r * nd + me] = sm3[j * own + r]
+            ar3[r * nd + slice_of(j)] = sm3[j * own + r]
         arrived(ar4.at[:, 0 : nd - 1, 0:12], r_row)
         rows = own * nd // 2
         lhs, rhs = slices(0, rows), slices(16, rows)
@@ -499,7 +558,7 @@
     sums = jnp.sum(bc[...], axis=0)
     zs[z] = sums
     r_sum = new_recv()
-    for k in sorted(range(1, gz), key=lambda k: -min(k, gz - k)):
+    for k in sorted(range(1, gz), key=lambda k: min(k, gz - k)):
         remote(zs.at[z], zs.at[z], r_sum, gz=wrapped(z + k, gz))
     for k in range(half):
         pol[:, 0, k, :] = bc[h * half + k]
@@ -528,7 +587,7 @@
         def vmem(*dims):
             return pltpu.VMEM((*dims, lanes), F32)
 
-        n_recv = 2 + 2 + 2 + 2 + 2 + 4 + 4 * (STEPS - 1) + 3
+        n_recv = 2 + 2 + 2 + 2 + 2 + 12 + 4 * (STEPS - 1) + 3
         polyakov, means = pl.pallas_call(
             functools.partial(kernel, ta, gz, half),
             out_shape=(
@@ -544,11 +603,16 @@
                 vmem(2, 3, 3, pad),
                 vmem(STEPS, 2, 2, 2, 2, 3, full),
                 vmem(2, 2, 2, 3, full),
-                vmem(4, 2, 2, 3, full),
+                vmem(2, 4, 2, 2, 3, full),
+                vmem(2, 2, 3, pad),
+                vmem(2, 2, 2, 3, half),
+                vmem(2, 16),
+                vmem(2, 16),
+                vmem(6, 2, 3, 3, half),
                 vmem(4, 2, 2, 3, full),
                 vmem(3, 2, 2, 3, pad),
                 vmem(2, 2, 3, 3, full),
-                vmem(6, 2, 2, 3, full),
+                vmem(6, 2, 2, 3, pad),
                 vmem(full * 16),
                 vmem(2 * full * 16),
                 vmem(18 * full),

time: 83.4 us -> 84.2 us (level)
  no operation moved by 1% of the time
where the time goes in v7:
time: 84.2 us; the launch traced here: 84 us
  Pallas kernels  82.2 us (98%)
  local copies, waits for them, and re-layouts  1.22 us (1%)
    pallas_call x1, Pallas kernels, body(): pl.pallas_call(functools.partial(kernel, ta, gz, half), out_shape=(jax.Sh...  82.2 us

profile of v7, /device:TPU:65, one launch (start us, length us, event | category | flops | bytes accessed | tf_op | source)
XLA Modules:
  0.0 84.0 jit_solution(17006638797660780299)
XLA Ops:
  0.6 82.2 %shard_map.41 = (f32[2,1,8,128]{3,2,1,0:T(8,128)S(1)}, f32[2,128]{1,0:T(2,128)S(1)}) custom-call(f32[3,2,3,3,2,1,8,128]{7,6,5,4,3,2,1,0:T(8,128)} %sp.1, f32[2,3,3,2,1,8,128]{6,5,4,3,2,1,0:T(8,128)} %tl.1), custom_call_target="tpu_custom_call" | custom-call | tf_op jit(solution)/shard_map/pallas_call | solution.py:591
  82.8 0.6 slice_reduce_fusion
  83.4 0.6 copy.5

commit v8 on v7

--- a/solution.py
+++ b/solution.py
@@ -202,7 +202,7 @@
         ready_x, ta // 2 - 1, [{"ta": wrapped(j + k, ta)} for k in sorted({1 % ta, ta - 1} - {0})]
     )
     hear_z = relay(
-        ready_z, gz // 2 - STEPS, [{"gz": wrapped(z + k, gz)} for k in sorted({1 % gz, gz - 1} - {0})]
+        ready_z, gz // 2 - 1, [{"gz": wrapped(z + k, gz)} for k in sorted({1 % gz, gz - 1} - {0})]
     )
 
     r_v, r_x, r_y, r_t = new_recv(2), new_recv(2), new_recv(2), new_recv(2)
@@ -226,6 +226,7 @@
     for t in range(2):
         remote(plane(None, t), two(TH, 0), r_t + h, gz=zm, gy=t)
     hear_x()
+    hear_z()
 
     def each_half(body):
         def run(k, carry):
@@ -320,6 +321,7 @@
     wrap(F, 0, FX)
     wrap(F, 0, FZ)
     in_plane(0)
+    hear_z()
     for k in range(2):
         arrived(F.at[0, FV, :, 0:2, :, halves[k]], r_v + k)
 
@@ -353,6 +355,9 @@
         last = s == STEPS - 1
         r_then = {f: new_recv(2) for f in (FX, FY)} if not last else {}
         for f in (FX, FY):
+            hear_z(last and f == FY)
+            if f == FY:
+                hear_x(last)
             for k in range(2):
                 arrived(H.at[s, :, f, :, :, :, halves[k]], r_now[f] + k)
                 across(s, f, k)
@@ -371,9 +376,6 @@
                 if last:
                     for k in range(2):
                         onward_row(s + 1, k)
-                hear_x(last)
-            if last:
-                hear_z()
             z_staples(s, f)
         r_now = r_then
         if s == 0:
@@ -381,9 +383,6 @@
             wrap(T)
             remote(T.at[:, 0:2, :, 0:full], TB.at[:, :, :, 0:full], r_tb, **beside[1])
         if s == STEPS - 2:
-            for t in range(2):
-                remote(plane(None, t), two(TH, 1), r_t + h, gz=zp, gy=t)
-
             @pl.when(h == 1)
             def _():
                 for side_k, to in ((0, zm), (1, zp)):
@@ -392,6 +391,9 @@
                             plane(None, t), THB.at[side_k], r_thb, cores=(1,),
                             ta=wrapped(j + t, ta), gz=to, gy=1 - t,
                         )
+
+            for t in range(2):
+                remote(plane(None, t), two(TH, 1), r_t + h, gz=zp, gy=t)
         z_links(s, last)
         if not last:
             in_plane(s + 1)
@@ -399,8 +401,6 @@
     n = STEPS
     r0, r1 = halves
     before1 = pl.ds(half - 1, half)
-    for k in range(2):
-        arrived(TH.at[:, :, :, :, halves[k]], r_t + k)
 
     def lower_y(rows, up):
         store(M, (3,), up, mul(load(F, (n, FY), rows), load(T, (), rows), da=True, rows=2))
@@ -412,21 +412,15 @@
     store(M, (0,), r0, mul(ux, ahead_x(t), rows=2))
     store(M, (1,), r0, mul(ux, t, da=True, rows=2))
     store(M, (2,), r0, mul(uy, load(T, (), pl.ds(1, half)), rows=2))
-    store(M, (4,), r0, mul(load(F, (n, FZ), r0), load2(TH, (0,), r0), rows=2))
-    store(M, (5,), r0, mul(load(F, (n, FV), r0), load2(TH, (1,), r0), da=True, rows=2))
 
     arrived(TB.at[:, :, :, 0:full], r_tb)
     wrap(TB)
-    arrived(THB, r_thb)
     t = load2(TB, (), r1)
     ux = load(F, (n, FX), r1)
     store(Q, (0,), r0, mul(ahead_x(t), ux, db=True))
     store(Q, (1,), r0, mul(t, ux))
     store(Q, (2,), r0, mul(load2(TB, (), pl.ds(half + 1, half)), load(F, (n, FY), r1), db=True))
     store(Q, (3,), r0, mul(load2(TB, (), before1), load(F, (n, FY), before1)))
-    store(Q, (4,), r0, mul(load2(THB, (0,), r0), load(F, (n, FZ), r1), db=True))
-    store(Q, (5,), r0, mul(load2(THB, (1,), r0), load(F, (n, FV), r1)))
-    hear_z()
 
     def came(k, f):
         arrived(UP.at[k, f, :, :, :, inner], r_next[k] + f)
@@ -457,8 +451,14 @@
                 mul(load2(UP, (1, FY), before1), load(Q, (3,), r0), da=True, rows=2),
             )
         store(S, (0,), halves[k], total)
-        if k == 0:
-            hear_z()
+
+    arrived(THB, r_thb)
+    store(Q, (4,), r0, mul(load2(THB, (0,), r0), load(F, (n, FZ), r1), db=True))
+    store(Q, (5,), r0, mul(load2(THB, (1,), r0), load(F, (n, FV), r1)))
+    for k in range(2):
+        arrived(TH.at[:, :, :, :, halves[k]], r_t + k)
+    store(M, (4,), r0, mul(load(F, (n, FZ), r0), load2(TH, (0,), r0), rows=2))
+    store(M, (5,), r0, mul(load(F, (n, FV), r0), load2(TH, (1,), r0), da=True, rows=2))
 
     for k in range(2):
         came(k, FZ)
@@ -505,8 +505,6 @@
     @pl.when(h == 0)
     def _():
         to_product(0, cores=(0,))
-
-    hear_z()
 
     def slices(start, rows):
         at = lambda c: ar[pl.ds(start + c, rows, 32), :]
@@ -554,7 +552,6 @@
     def _():
         arrived(bc, r_out)
 
-    hear_z(True)
     sums = jnp.sum(bc[...], axis=0)
     zs[z] = sums
     r_sum = new_recv()

time: 84.2 us -> 82.3 us (0.977)
  Pallas kernels: 82.2 us -> 80.3 us
    pallas_call x1, Pallas kernels: 82.2 us -> 80.3 us  [body(): pl.pallas_call(functools.partial(kernel, ta, gz, half), out_shape=(jax.Sh...]
where the time goes in v8:
time: 82.3 us; the launch traced here: 82.2 us
  Pallas kernels  80.3 us (98%)
  local copies, waits for them, and re-layouts  1.22 us (1%)
    pallas_call x1, Pallas kernels, body(): pl.pallas_call(functools.partial(kernel, ta, gz, half), out_shape=(jax.Sh...  80.3 us

profile of v8, /device:TPU:65, one launch (start us, length us, event | category | flops | bytes accessed | tf_op | source)
XLA Modules:
  0.0 82.2 jit_solution(15790889698915652745)
XLA Ops:
  0.6 80.3 %shard_map.41 = (f32[2,1,8,128]{3,2,1,0:T(8,128)S(1)}, f32[2,128]{1,0:T(2,128)S(1)}) custom-call(f32[3,2,3,3,2,1,8,128]{7,6,5,4,3,2,1,0:T(8,128)} %sp.1, f32[2,3,3,2,1,8,128]{6,5,4,3,2,1,0:T(8,128)} %tl.1), custom_call_target="tpu_custom_call" | custom-call | tf_op jit(solution)/shard_map/pallas_call | solution.py:588
  81.0 0.6 slice_reduce_fusion
  81.6 0.6 copy.5

commit v9 on v8

--- a/solution.py
+++ b/solution.py
@@ -182,28 +182,28 @@
     near[0].wait()
     pl.semaphore_wait(barrier, 1 + 2 * len(around))
 
-    def relay(sem, rounds, sides):
-        done = [0]
-
-        def go(last=False):
-            while True:
-                if 0 < done[0] <= rounds:
-                    pl.semaphore_wait(sem.at[done[0] - 1], len(sides))
-                done[0] += 1
-                if done[0] <= rounds:
-                    for where in sides:
-                        signal(sem.at[done[0] - 1], **where)
-                if not last or done[0] > rounds:
-                    return
+    def relay(sem, axis, here, size):
+        reach = [1]
+        waiting = [None]
+
+        def go():
+            if waiting[0] is not None:
+                pl.semaphore_wait(sem.at[waiting[0][0]], waiting[0][1])
+                waiting[0] = None
+            if 2 * reach[0] <= size:
+                n = reach[0]
+                sides = sorted({n % size, (size - n) % size} - {0})
+                if n < size // 2:
+                    index = n.bit_length() - 1
+                    for k in sides:
+                        signal(sem.at[index], **{axis: wrapped(here + k, size)})
+                    waiting[0] = (index, len(sides))
+                    reach[0] = 2 * n
 
         return go
 
-    hear_x = relay(
-        ready_x, ta // 2 - 1, [{"ta": wrapped(j + k, ta)} for k in sorted({1 % ta, ta - 1} - {0})]
-    )
-    hear_z = relay(
-        ready_z, gz // 2 - 1, [{"gz": wrapped(z + k, gz)} for k in sorted({1 % gz, gz - 1} - {0})]
-    )
+    hear_x = relay(ready_x, "ta", j, ta)
+    hear_z = relay(ready_z, "gz", z, gz)
 
     r_v, r_x, r_y, r_t = new_recv(2), new_recv(2), new_recv(2), new_recv(2)
     r_own, r_ownt = new_recv(), new_recv()
@@ -262,7 +262,11 @@
     def side(ref, s, f, rows, up):
         return ahead_x(load(ref, (s, f), rows)) if up is None else load(ref, (s, f), up)
 
-    def across(s, f, k):
+    def span(k):
+        r0 = pl.multiple_of(k * half, half)
+        return pl.ds(r0, half), pl.ds(r0 + 1, half)
+
+    def across(s, f, rows, up):
         def body(rows, up):
             up = None if f == FX else up
             uz, uz_f = load(F, (s, FZ), rows), side(F, s, FZ, rows, up)
@@ -277,7 +281,7 @@
                 total = add(total, load(L, (0,), rows, 2))
             store(F, (s + 1, f), rows, mixed(load(F, (s, f), rows, 2), total, 0.125))
 
-        body(halves[k], pl.ds(k * half + 1, half))
+        body(rows, up)
 
     def z_staples(s, f):
         def body(rows, up):
@@ -304,13 +308,13 @@
             unwrap(2)
 
     def z_links(s, last):
-        for f, k in ((FZ, 1), (FV, 2)):
-            for part in range(2):
-                rows = halves[part]
+        for part in (h, o):
+            rows, _ = span(part)
+            for f, k in ((FZ, 1), (FV, 2)):
                 total = add(load(S, (f,), rows, 2), load(L, (k,), rows, 2))
                 store(F, (s + 1, f), rows, mixed(load(F, (s, f), rows, 2), total, 0.125))
                 if last:
-                    onward(s + 1, f, part)
+                    onward(s + 1, f, part, rows)
         wrap(F, s + 1, FZ)
         wrap(F, s + 1, FV)
 
@@ -321,7 +325,6 @@
     wrap(F, 0, FX)
     wrap(F, 0, FZ)
     in_plane(0)
-    hear_z()
     for k in range(2):
         arrived(F.at[0, FV, :, 0:2, :, halves[k]], r_v + k)
 
@@ -331,14 +334,15 @@
     each_half(complete)
     wrap(F, 0, FV)
 
-    r_next = [new_recv(5), new_recv(5)]
+    r_next = new_recv(10)
     r_tb, r_thb = new_recv(), new_recv()
     beside = [{"ta": wrapped(j + h + ta - 1, ta), "gy": o}, {"ta": wrapped(j + h, ta), "gy": o}]
     inner = pl.ds(half, half)
 
-    def onward(s, f, k):
+    def onward(s, f, k, rows):
+        to = {"ta": jnp.where(k == 0, beside[0]["ta"], beside[1]["ta"]), "gy": o}
         remote(
-            F.at[s, f, :, 0:2, :, halves[k]], UP.at[k, f, :, :, :, inner], r_next[k] + f, **beside[k]
+            F.at[s, f, :, 0:2, :, rows], UP.at[k, f, :, :, :, inner], r_next + 5 * k + f, **to
         )
 
     def entries():
@@ -348,27 +352,25 @@
         row = full - 1 if k == 0 else half - 1
         for c, (part, a, b) in enumerate(entries()):
             YP[k, pl.ds(c, 1), :] = F[s, FY, part, a, b, pl.ds(row, 1), :]
-        remote(YP.at[k, 0:12], YQ.at[k, 0:12], r_next[k] + 4, **beside[k])
+        remote(YP.at[k, 0:12], YQ.at[k, 0:12], r_next + 5 * k + 4, **beside[k])
 
     r_now = {FX: r_x, FY: r_y}
     for s in range(STEPS):
         last = s == STEPS - 1
         r_then = {f: new_recv(2) for f in (FX, FY)} if not last else {}
         for f in (FX, FY):
-            hear_z(last and f == FY)
-            if f == FY:
-                hear_x(last)
-            for k in range(2):
-                arrived(H.at[s, :, f, :, :, :, halves[k]], r_now[f] + k)
-                across(s, f, k)
+            (hear_z if f == FX else hear_x)()
+            for k in (h, o):
+                rows, up = span(k)
+                arrived(H.at[s, :, f, :, :, :, rows], r_now[f] + k)
+                across(s, f, rows, up)
                 if last:
-                    onward(s + 1, f, k)
+                    onward(s + 1, f, k, rows)
                 else:
-                    out = F.at[s + 1, f, :, 0:2, :, halves[k]]
+                    out = F.at[s + 1, f, :, 0:2, :, rows]
                     for side_k, to in ((0, zm), (1, zp)):
                         remote(
-                            out, H.at[s + 1, side_k, f, :, :, :, halves[k]],
-                            r_then[f] + k, gz=to,
+                            out, H.at[s + 1, side_k, f, :, :, :, rows], r_then[f] + k, gz=to
                         )
             if f == FX:
                 wrap(F, s + 1, FX)
@@ -423,10 +425,10 @@
     store(Q, (3,), r0, mul(load2(TB, (), before1), load(F, (n, FY), before1)))
 
     def came(k, f):
-        arrived(UP.at[k, f, :, :, :, inner], r_next[k] + f)
+        arrived(UP.at[k, f, :, :, :, inner], r_next + 5 * k + f)
 
     def row_came(k):
-        arrived(YQ.at[k, 0:12], r_next[k] + 4)
+        arrived(YQ.at[k, 0:12], r_next + 5 * k + 4)
         for c, (part, a, b) in enumerate(entries()):
             UP[k, FY, part, a, b, pl.ds(half - 1, 1), :] = YQ[k, pl.ds(c, 1), :]
 

time: 82.3 us -> 82.3 us (level)
  no operation moved by 1% of the time
where the time goes in v9:
time: 82.3 us; the launch traced here: 82.1 us
  Pallas kernels  80.3 us (98%)
  local copies, waits for them, and re-layouts  1.22 us (1%)
    pallas_call x1, Pallas kernels, body(): pl.pallas_call(functools.partial(kernel, ta, gz, half), out_shape=(jax.Sh...  80.3 us

profile of v9, /device:TPU:65, one launch (start us, length us, event | category | flops | bytes accessed | tf_op | source)
XLA Modules:
  0.0 82.1 jit_solution(4760457818935930338)
XLA Ops:
  0.6 80.3 %shard_map.41 = (f32[2,1,8,128]{3,2,1,0:T(8,128)S(1)}, f32[2,128]{1,0:T(2,128)S(1)}) custom-call(f32[3,2,3,3,2,1,8,128]{7,6,5,4,3,2,1,0:T(8,128)} %sp.1, f32[2,3,3,2,1,8,128]{6,5,4,3,2,1,0:T(8,128)} %tl.1), custom_call_target="tpu_custom_call" | custom-call | tf_op jit(solution)/shard_map/pallas_call | solution.py:590
  80.9 0.6 slice_reduce_fusion
  81.5 0.6 copy.5

commit v10 on v9

--- a/solution.py
+++ b/solution.py
@@ -432,11 +432,11 @@
         for c, (part, a, b) in enumerate(entries()):
             UP[k, FY, part, a, b, pl.ds(half - 1, 1), :] = YQ[k, pl.ds(c, 1), :]
 
-    for k in range(2):
-        came(k, FX)
-        came(k, FY)
-        row_came(k)
-        if k == 0:
+    def first_half(part):
+        if part == 0:
+            came(0, FX)
+            came(0, FY)
+            row_came(0)
             ux = load2(UP, (0, FX), inner)
             total = add(
                 mul(load(M, (0,), r0, 2), ux, db=True, rows=2),
@@ -444,7 +444,26 @@
                 mul(load(M, (2,), r0, 2), load2(UP, (0, FY), inner), db=True, rows=2),
                 mul(load(M, (3,), r0, 2), load2(UP, (0, FY), before1), rows=2),
             )
+            store(S, (0,), r0, total)
+            for k in range(2):
+                arrived(TH.at[:, :, :, :, halves[k]], r_t + k)
+            store(M, (4,), r0, mul(load(F, (n, FZ), r0), load2(TH, (0,), r0), rows=2))
+            store(M, (5,), r0, mul(load(F, (n, FV), r0), load2(TH, (1,), r0), da=True, rows=2))
         else:
+            came(0, FZ)
+            came(0, FV)
+            total = add(
+                load(S, (0,), r0, 2),
+                mul(load(M, (4,), r0, 2), load2(UP, (0, FZ), inner), db=True, rows=2),
+                mul(load(M, (5,), r0, 2), load2(UP, (0, FV), inner), rows=2),
+            )
+            smoothed(0, load(T, (), r0, 2), total)
+
+    def second_half(part):
+        if part == 0:
+            came(1, FX)
+            came(1, FY)
+            row_came(1)
             ux = load2(UP, (1, FX), inner)
             total = add(
                 mul(ux, load(Q, (0,), r0), rows=2),
@@ -452,34 +471,21 @@
                 mul(load2(UP, (1, FY), inner), load(Q, (2,), r0), rows=2),
                 mul(load2(UP, (1, FY), before1), load(Q, (3,), r0), da=True, rows=2),
             )
-        store(S, (0,), halves[k], total)
-
-    arrived(THB, r_thb)
-    store(Q, (4,), r0, mul(load2(THB, (0,), r0), load(F, (n, FZ), r1), db=True))
-    store(Q, (5,), r0, mul(load2(THB, (1,), r0), load(F, (n, FV), r1)))
-    for k in range(2):
-        arrived(TH.at[:, :, :, :, halves[k]], r_t + k)
-    store(M, (4,), r0, mul(load(F, (n, FZ), r0), load2(TH, (0,), r0), rows=2))
-    store(M, (5,), r0, mul(load(F, (n, FV), r0), load2(TH, (1,), r0), da=True, rows=2))
-
-    for k in range(2):
-        came(k, FZ)
-        came(k, FV)
-        uz, uv = load2(UP, (k, FZ), inner), load2(UP, (k, FV), inner)
-        if k == 0:
-            link = load(T, (), r0, 2)
-            total = add(
-                load(S, (0,), r0, 2),
-                mul(load(M, (4,), r0, 2), uz, db=True, rows=2),
-                mul(load(M, (5,), r0, 2), uv, rows=2),
-            )
+            store(S, (0,), r1, total)
+            arrived(THB, r_thb)
+            store(Q, (4,), r0, mul(load2(THB, (0,), r0), load(F, (n, FZ), r1), db=True))
+            store(Q, (5,), r0, mul(load2(THB, (1,), r0), load(F, (n, FV), r1)))
         else:
-            link = load(TB, (), r1, 2)
+            came(1, FZ)
+            came(1, FV)
             total = add(
                 load(S, (0,), r1, 2),
-                mul(uz, load(Q, (4,), r0), rows=2),
-                mul(uv, load(Q, (5,), r0), da=True, rows=2),
+                mul(load2(UP, (1, FZ), inner), load(Q, (4,), r0), rows=2),
+                mul(load2(UP, (1, FV), inner), load(Q, (5,), r0), da=True, rows=2),
             )
+            smoothed(1, load(TB, (), r1, 2), total)
+
+    def smoothed(k, link, total):
         done = mixed(link, total, 0.5 / 6.0)
         for c, (part, a, b) in enumerate(entries()):
             sm[pl.ds(k * half * 16 + c, half, 16), :] = done[part][a][b]
@@ -494,19 +500,41 @@
     def slice_of(jd):
         return jnp.where(jd * own < half, me, wrapped(me + nd - 1, nd))
 
-    def to_product(k, **kw):
-        jd = wrapped(j + k, ta) if k else j
-        remote(
-            sm3.at[pl.ds(jd * own, own), 0:12], ar4.at[:, slice_of(jd), 0:12], r_row,
-            ta=jd, gy=1, **kw,
-        )
-
-    for k in away:
-        to_product(k)
+    def to_products(k, c):
+        here, part = wrapped(j, ta // 2), ta // 2
+        for i in range(part):
+            jd = k * part + wrapped(here + i, part)
+
+            def go(jd=jd):
+                remote(
+                    sm3.at[pl.ds(jd * own, own), 0:12], ar4.at[:, slice_of(jd), 0:12], r_row,
+                    cores=(c,), ta=jd, gy=1,
+                )
+
+            if c == 0:
+                go()
+            else:
+                pl.when(jd != j)(go)
 
     @pl.when(h == 0)
     def _():
-        to_product(0, cores=(0,))
+        first_half(0)
+        first_half(1)
+        to_products(0, 0)
+        second_half(0)
+        second_half(1)
+        to_products(1, 0)
+
+    @pl.when(h == 1)
+    def _():
+        second_half(0)
+        second_half(1)
+        to_products(1, 1)
+        first_half(0)
+        first_half(1)
+        to_products(0, 1)
+
+    rows_sent[1] -= own * 12
 
     def slices(start, rows):
         at = lambda c: ar[pl.ds(start + c, rows, 32), :]
@@ -564,7 +592,9 @@
     arrived(zs.at[pl.ds(0, gz - 1)], r_sum)
     totals = jnp.sum(zs[...], axis=0)
     sites = float(full * gz * sp.shape[-1])
-    mean[...] = jnp.broadcast_to(jnp.sum(totals, axis=1, keepdims=True) / sites, totals.shape)
+    totals = jnp.sum(totals, axis=1, keepdims=True) / sites
+    lane = lax.broadcasted_iota(jnp.int32, (1, lanes), 1)
+    mean[...] = jnp.where(lane == 0, totals[0:1], totals[1:2])
 
     def all_sent(c):
         lines = F.reshape(math.prod(F.shape[:-1]), lanes).at[pl.ds(0, rows_sent[c])]
@@ -572,6 +602,11 @@
 
     for c in range(2):
         pl.when(h == c)(functools.partial(all_sent, c))
+
+
+def write_out(polyakov, means, polyakov_out, means_out):
+    polyakov_out[...] = polyakov[...]
+    means_out[...] = means[0, 0:2]
 
 
 def solution(mesh):
@@ -591,7 +626,7 @@
             functools.partial(kernel, ta, gz, half),
             out_shape=(
                 jax.ShapeDtypeStruct((2, 1, half, lanes), F32),
-                jax.ShapeDtypeStruct((2, lanes), F32),
+                jax.ShapeDtypeStruct((1, lanes), F32),
             ),
             in_specs=[pl.BlockSpec(memory_space=pltpu.HBM)] * 2,
             out_specs=(pl.BlockSpec(memory_space=pltpu.VMEM),) * 2,
@@ -628,7 +663,16 @@
                 collective_id=0, has_side_effects=True, vmem_limit_bytes=56_450_000
             ),
         )(sp, tl)
-        return polyakov, means[:, 0]
+        return pl.pallas_call(
+            write_out,
+            out_shape=(
+                jax.ShapeDtypeStruct(polyakov.shape, F32),
+                jax.ShapeDtypeStruct((2,), F32),
+            ),
+            in_specs=[pl.BlockSpec(memory_space=pltpu.VMEM)] * 2,
+            out_specs=(pl.BlockSpec(memory_space=pltpu.VMEM),) * 2,
+            compiler_params=pltpu.CompilerParams(vmem_limit_bytes=1024 * 1024),
+        )(polyakov, means)
 
     return jax.shard_map(
         body,

time: 82.3 us -> 81.5 us (level)
  local copies, waits for them, and re-layouts: 1.22 us -> 0 us
where the time goes in v10:
time: 81.5 us; the launch traced here: 81.4 us
  Pallas kernels  80.7 us (99%)
    pallas_call x1, Pallas kernels, body(): pl.pallas_call(functools.partial(kernel, ta, gz, half), out_shape=(jax.Sh...  80.1 us

profile of v10, /device:TPU:65, one launch (start us, length us, event | category | flops | bytes accessed | tf_op | source)
XLA Modules:
  0.0 81.4 jit_solution(2399086031607060341)
XLA Ops:
  0.6 80.1 %shard_map.41 = (f32[2,1,8,128]{3,2,1,0:T(8,128)S(1)}, f32[1,128]{1,0:T(1,128)S(1)}) custom-call(f32[3,2,3,3,2,1,8,128]{7,6,5,4,3,2,1,0:T(8,128)} %sp.1, f32[2,3,3,2,1,8,128]{6,5,4,3,2,1,0:T(8,128)} %tl.1), custom_call_target="tpu_custom_call" | custom-call | tf_op jit(solution)/shard_map/pallas_call | solution.py:625
  80.8 0.6 shard_map.42

commit v11 on v10

--- a/solution.py
+++ b/solution.py
@@ -216,11 +216,13 @@
 
     for t in range(2):
         remote(plane(FZ, t), two(F, 0, FV), r_v + h, gz=zp, gy=t)
-    remote(SP.at[:, :, :, :, o, 0], F.at[0, 0:3, :, :, :, mine], r_own, gy=o)
-    for f, r in ((FX, r_x), (FY, r_y)):
-        for t in range(2):
-            remote(plane(f, t), two(H, 0, 0, f), r + h, gz=zm, gy=t)
-            remote(plane(f, t), two(H, 0, 1, f), r + h, gz=zp, gy=t)
+        remote(plane(FX, t), two(H, 0, 0, FX), r_x + h, gz=zm, gy=t)
+        remote(plane(FX, t), two(H, 0, 1, FX), r_x + h, gz=zp, gy=t)
+        if t == 0:
+            remote(SP.at[:, :, :, :, o, 0], F.at[0, 0:3, :, :, :, mine], r_own, gy=o)
+    for t in range(2):
+        remote(plane(FY, t), two(H, 0, 0, FY), r_y + h, gz=zm, gy=t)
+        remote(plane(FY, t), two(H, 0, 1, FY), r_y + h, gz=zp, gy=t)
     near[1].wait()
     remote(TL.at[:, :, :, o, 0], T.at[:, :, :, mine], r_ownt, gy=o)
     for t in range(2):

time: 81.5 us -> 81.5 us (level)
  no operation moved by 1% of the time
where the time goes in v11:
time: 81.5 us; the launch traced here: 81.4 us
  Pallas kernels  80.8 us (99%)
    pallas_call x1, Pallas kernels, body(): pl.pallas_call(functools.partial(kernel, ta, gz, half), out_shape=(jax.Sh...  80.1 us

profile of v11, /device:TPU:65, one launch (start us, length us, event | category | flops | bytes accessed | tf_op | source)
XLA Modules:
  0.0 81.4 jit_solution(11818803479039346968)
XLA Ops:
  0.6 80.1 %shard_map.41 = (f32[2,1,8,128]{3,2,1,0:T(8,128)S(1)}, f32[1,128]{1,0:T(1,128)S(1)}) custom-call(f32[3,2,3,3,2,1,8,128]{7,6,5,4,3,2,1,0:T(8,128)} %sp.1, f32[2,3,3,2,1,8,128]{6,5,4,3,2,1,0:T(8,128)} %tl.1), custom_call_target="tpu_custom_call" | custom-call | tf_op jit(solution)/shard_map/pallas_call | solution.py:627
  80.8 0.6 shard_map.42
